TPU v7x, 32 devices: a whole 2x2x4 slice. The times are simulated.
32 devices in a mesh: tm: 4 (over x, core), space: 8 (over z, y).
Axes of the slice: x: 2, y: 2, z: 4, core: 2. Of those that a mesh axis runs over, the one named last changes fastest.
Arguments:
- initial_state: float32 [512, 3, 512], P('space'), may hold values from -1 to 1, as said below
- applied_field: float32 [512, 3, 512], P('space'), may hold values from -2 to 2
- coupling: float32 [512, 512], P('space'), may hold values from 0.5 to 2
Outputs:
- slice_states: float32 [4, 512, 3, 512], P('tm', 'space')
Inputs may be any that keep to these rules, and one draw needn't show every extreme that they name: `initial_state`: every cell's three components form a vector of length one.
All inputs are finite; a program needn't handle non-finite values.
Results may differ from a plain program's by a relative error of at most 0.00014.
Values sent between devices are 32-bit elements; how exact they have to be, the bound alone decides.
A program may use at most 128 MiB of HBM per device.

v0:
```python
import math

import jax
import jax.numpy as jnp
import numpy as np
from jax import lax
from jax.experimental import pallas as pl
from jax.experimental.pallas import tpu as pltpu
from jax.sharding import Mesh, PartitionSpec as P

FINE = 2
step_time = 0.06
damping = 0.02
stiffness = 0.25
thickness = 8.0

RING = ("core", "rest")
LOCAL = ("core", "zh", "rest")
EVERY = ("x", "core", "zh", "rest")


def real_tables(grid, parts):
    length = 2 * grid
    place = np.arange(grid)
    wave = np.arange(grid)
    angle = 2.0 * np.pi / length * ((place[:, None] * wave[None, :]) % length)
    cosine, sine = np.cos(angle), np.sin(angle)
    sine[:, 0] = 1.0 - 2.0 * (place % 2)
    width = grid // parts
    tall = np.concatenate([cosine, sine], axis=1).astype(np.float32)
    blocks = np.stack([cosine.reshape(grid, parts, width), sine.reshape(grid, parts, width)], axis=2)
    return tall, blocks.reshape(grid, length).astype(np.float32)


def spectral_tensor(rows, columns, length):
    wave_rows = 2.0 * math.pi / length * rows.astype(jnp.float32)
    wave_columns = 2.0 * math.pi / length * columns.astype(jnp.float32)
    squared = wave_rows * wave_rows + wave_columns * wave_columns
    nonzero = squared > 0.0
    safe = jnp.where(nonzero, squared, 1.0)
    scaled = jnp.sqrt(safe) * thickness
    film = jnp.where(nonzero, (1.0 - jnp.exp(-scaled)) / scaled, 1.0)
    in_plane = (1.0 - film) / safe
    half = length // 2
    edge_row = (rows == 0) | (rows == half)
    edge_column = (columns == 0) | (columns == half)
    weight = jnp.where(edge_row, 1.0, 2.0) * jnp.where(edge_column, 1.0, 2.0) * (-1.0 / (length * length))
    return (
        in_plane * wave_columns * wave_columns * weight,
        in_plane * wave_rows * wave_rows * weight,
        jnp.where(edge_row | edge_column, 0.0, in_plane * wave_columns * wave_rows * weight),
        film * weight,
    )


def exchange_field(padded, pad_coupling):
    center = padded[:, 1:-1]
    coupling = pad_coupling[1:-1]
    wide = jnp.pad(padded[:, 1:-1], ((0, 0), (0, 0), (1, 1)))
    wide_coupling = jnp.pad(coupling, ((0, 0), (1, 1)))
    total = pad_coupling[2:] * (padded[:, 2:] - center)
    total = total + pad_coupling[:-2] * (padded[:, :-2] - center)
    total = total + wide_coupling[:, 2:] * (wide[:, :, 2:] - center)
    total = total + wide_coupling[:, :-2] * (wide[:, :, :-2] - center)
    return stiffness * coupling * total


def cross(a, b):
    return jnp.stack([a[1] * b[2] - a[2] * b[1], a[2] * b[0] - a[0] * b[2], a[0] * b[1] - a[1] * b[0]])


def torque(magnet, effective):
    first = cross(magnet, effective)
    return -(first + damping * cross(magnet, first)) * (1.0 / (1.0 + damping * damping))


def coarse(padded, pad_coupling, field):
    center = padded[:, 1:-1]
    effective = exchange_field(padded, pad_coupling) + field
    effective = jnp.stack([effective[0], effective[1], effective[2] - center[2]])
    return center + FINE * step_time * torque(center, effective)


def dot(left, right):
    return jnp.dot(left, right, precision=lax.Precision.HIGH)


def halves(table):
    high = table.astype(jnp.bfloat16)
    return [high, (table - high.astype(np.float32)).astype(jnp.bfloat16)]


def split(value):
    high = value.astype(jnp.bfloat16)
    return high, (value - high.astype(jnp.float32)).astype(jnp.bfloat16)


def dot3(left_high, left_low, right_high, right_low):
    def one(a, b):
        return jnp.dot(a, b, preferred_element_type=jnp.float32)

    return one(left_high, right_high) + (one(left_high, right_low) + one(left_low, right_high))


def fine_kernel(
    space,
    start, field, links, coarse_end, tensors,
    cut_high, cut_low, up_high, up_low, tall_high, tall_low, back_high, back_low,
    out,
    current, rate, base, edge_out, edge_in, send, got, send_back, got_back,
    columns_high, columns_low, mixed_high, mixed_low, wide_high, wide_low, demag,
    edge_sems, send_sems, got_sems, send_back_sems, got_back_sems,
):
    _, rows, grid = start.shape
    rest = space // 2
    width = 2 * grid // space
    part = lax.axis_index("core") * rest + lax.axis_index("rest")

    def device(target):
        return {"core": target // rest, "rest": target % rest}

    barrier = pltpu.get_barrier_semaphore()

    def greet(k, carry):
        pl.semaphore_signal(
            barrier, inc=1, device_id=device((part + k) % space), device_id_type=pl.DeviceIdType.MESH
        )
        return carry

    lax.fori_loop(1, space, greet, 0)
    pl.semaphore_wait(barrier, space - 1)

    def remote(source, target, send_sem, recv_sem, where):
        return pltpu.make_async_remote_copy(
            src_ref=source, dst_ref=target, send_sem=send_sem, recv_sem=recv_sem,
            device_id=device(where), device_id_type=pl.DeviceIdType.MESH,
        )

    def forward(k):
        target = (part + k) % space
        return remote(send.at[target], got.at[part], send_sems.at[k], got_sems.at[k], target)

    def backward(k):
        target = (part + k) % space
        return remote(
            send_back.at[target], got_back.at[part], send_back_sems.at[k], got_back_sems.at[k], target
        )

    current[:, 8 : 8 + rows, :] = start[...]
    base[...] = start[...]

    def evaluate(parity):
        for c in range(3):
            edge_out[0, c : c + 1, :] = current[c, 8:9, :]
            edge_out[1, c : c + 1, :] = current[c, 7 + rows : 8 + rows, :]
        magnet_high, magnet_low = split(current[:, 8 : 8 + rows, :].reshape(3 * rows, grid))
        wide_high[:, :grid] = magnet_high
        wide_low[:, :grid] = magnet_low

        def block(index):
            return dot3(wide_high[:, :grid], wide_low[:, :grid], cut_high[index], cut_low[index])

        to_before = remote(
            edge_out.at[0], edge_in.at[parity, 1], edge_sems.at[0], edge_sems.at[1], (part + space - 1) % space
        )
        to_after = remote(
            edge_out.at[1], edge_in.at[parity, 0], edge_sems.at[2], edge_sems.at[3], (part + 1) % space
        )
        to_before.start()
        to_after.start()

        def push(k, carry):
            target = (part + k) % space
            send[target] = block(target)
            forward(k).start()
            return carry

        lax.fori_loop(1, space, push, 0)
        got[part] = block(part)

        def take(k, carry):
            forward(k).wait()
            return carry

        lax.fori_loop(1, space, take, 0)
        to_before.wait()
        to_after.wait()
        for c in range(3):
            current[c, 7:8, :] = edge_in[parity, 0, c : c + 1, :]
            current[c, 8 + rows : 9 + rows, :] = edge_in[parity, 1, c : c + 1, :]
        columns = jnp.concatenate(
            [got[:, c * rows : (c + 1) * rows, :].reshape(grid, width) for c in range(3)], axis=1
        )
        columns_high[...], columns_low[...] = split(columns)

        step = grid // 2

        def mix(i, carry):
            lower = pl.multiple_of(i * step, step)
            upper = pl.multiple_of(grid + i * step, step)

            def spectrum(at):
                return dot3(
                    up_high[pl.ds(at, step), :], up_low[pl.ds(at, step), :], columns_high[...], columns_low[...]
                )

            pair = (spectrum(lower), spectrum(upper))
            for q, at in enumerate((lower, upper)):
                txx, tyy, txy, tzz = (tensors[n, pl.ds(at, step), :] for n in range(4))
                sx, sy, sz = (pair[q][:, c * width : (c + 1) * width] for c in range(3))
                ox, oy = (pltpu.roll(pair[1 - q][:, c * width : (c + 1) * width], width // 2, 1) for c in range(2))
                for c, value in enumerate((txx * sx + txy * oy, txy * ox + tyy * sy, tzz * sz)):
                    high, low = split(value)
                    mixed_high[pl.ds(at, step), c * width : (c + 1) * width] = high
                    mixed_low[pl.ds(at, step), c * width : (c + 1) * width] = low
            return carry

        lax.fori_loop(0, 2, mix, 0)

        def synth(i, carry):
            at = pl.multiple_of(i * step, step)
            value = dot3(
                tall_high[pl.ds(at, step), :], tall_low[pl.ds(at, step), :], mixed_high[...], mixed_low[...]
            )
            send_back[pl.ds(i * (space // 2), space // 2)] = value.reshape(space // 2, rows, 3 * width)

            def push_back(j, inner):
                target = i * (space // 2) + j

                @pl.when(target != part)
                def _():
                    backward((target - part + space) % space).start()

                return inner

            return lax.fori_loop(0, space // 2, push_back, carry)

        lax.fori_loop(0, 2, synth, 0)

        got_back[part] = send_back[part]

        def take_back(k, carry):
            backward(k).wait()
            return carry

        lax.fori_loop(1, space, take_back, 0)
        for j in range(space):
            for c in range(3):
                high, low = split(got_back[j, :, c * width : (c + 1) * width])
                wide_high[c * rows : (c + 1) * rows, j * width : (j + 1) * width] = high
                wide_low[c * rows : (c + 1) * rows, j * width : (j + 1) * width] = low
        demag[...] = dot3(wide_high[...], wide_low[...], back_high[...], back_low[...])

        for at in range(0, rows, 8):
            inside = [current[c, 8 + at : 16 + at, :] for c in range(3)]
            weights = [links[n, at : at + 8, :] for n in range(4)]
            effective = []
            for c in range(3):
                m = inside[c]
                total = weights[0] * (current[c, 7 + at : 15 + at, :] - m)
                total = total + weights[1] * (current[c, 9 + at : 17 + at, :] - m)
                total = total + weights[2] * (pltpu.roll(m, 1, 1) - m)
                total = total + weights[3] * (pltpu.roll(m, grid - 1, 1) - m)
                effective.append(total + demag[c * rows + at : c * rows + at + 8, :] + field[c, at : at + 8, :])
            first = cross_of(inside, effective)
            second = cross_of(inside, first)
            for c in range(3):
                value = -(first[c] + damping * second[c]) * (1.0 / (1.0 + damping * damping))
                if parity == 0:
                    rate[c, at : at + 8, :] = value
                else:
                    moved = base[c, at : at + 8, :] + 0.5 * step_time * (rate[c, at : at + 8, :] + value)
                    base[c, at : at + 8, :] = moved
        if parity == 0:
            current[:, 8 : 8 + rows, :] = base[...] + step_time * rate[...]
        else:
            current[:, 8 : 8 + rows, :] = base[...]

    def fine_step(i, carry):
        evaluate(0)
        evaluate(1)
        return carry

    lax.fori_loop(0, FINE, fine_step, 0)
    out[...] = base[...] - coarse_end[...]


def cross_of(a, b):
    return [a[1] * b[2] - a[2] * b[1], a[2] * b[0] - a[0] * b[2], a[0] * b[1] - a[1] * b[0]]


def fine_jump(space, start, field, links, coarse_end, tensors, tables):
    _, rows, grid = start.shape
    length = 2 * grid
    width = length // space

    def kernel(*refs):
        fine_kernel(space, *refs)

    f32, bf16 = jnp.float32, jnp.bfloat16
    operands = [start, field, links, coarse_end, tensors, *tables]
    return pl.pallas_call(
        kernel,
        out_shape=jax.ShapeDtypeStruct(start.shape, f32),
        in_specs=[pl.BlockSpec(memory_space=pltpu.VMEM)] * len(operands),
        out_specs=pl.BlockSpec(memory_space=pltpu.VMEM),
        scratch_shapes=[
            pltpu.VMEM((3, rows + 16, grid), f32),
            pltpu.VMEM((3, rows, grid), f32),
            pltpu.VMEM((3, rows, grid), f32),
            pltpu.VMEM((2, 8, grid), f32),
            pltpu.VMEM((2, 2, 8, grid), f32),
            pltpu.VMEM((space, 3 * rows, width), f32),
            pltpu.VMEM((space, 3 * rows, width), f32),
            pltpu.VMEM((space, rows, 3 * width), f32),
            pltpu.VMEM((space, rows, 3 * width), f32),
            pltpu.VMEM((grid, 3 * width), bf16),
            pltpu.VMEM((grid, 3 * width), bf16),
            pltpu.VMEM((length, 3 * width), bf16),
            pltpu.VMEM((length, 3 * width), bf16),
            pltpu.VMEM((3 * rows, length), bf16),
            pltpu.VMEM((3 * rows, length), bf16),
            pltpu.VMEM((3 * rows, grid), f32),
            pltpu.SemaphoreType.DMA((4,)),
            pltpu.SemaphoreType.DMA((space,)),
            pltpu.SemaphoreType.DMA((space,)),
            pltpu.SemaphoreType.DMA((space,)),
            pltpu.SemaphoreType.DMA((space,)),
        ],
        compiler_params=pltpu.CompilerParams(
            collective_id=0, has_side_effects=True, vmem_limit_bytes=56 * 1024 * 1024
        ),
    )(*operands)


def links_of(pad_coupling, depth):
    rows = pad_coupling.shape[0] - 2 * depth
    own = pad_coupling[depth : rows + depth]
    flat = jnp.pad(own, ((0, 0), (1, 1)))
    around = [
        pad_coupling[depth - 1 : rows + depth - 1],
        pad_coupling[depth + 1 : rows + depth + 1],
        flat[:, :-2],
        flat[:, 2:],
    ]
    return stiffness * own[None] * jnp.stack(around)


def sweep_kernel(
    space, tm, jump, opening, field, links, out,
    current, landed, edge_out, edge_in, swap_sems, send_sems, recv_sems,
):
    _, rows, grid = opening.shape
    rest = space // 2
    core, zh = lax.axis_index("core"), lax.axis_index("zh")
    number = lax.axis_index("x") * 2 + core
    place = zh * rest + lax.axis_index("rest")
    mesh_type = pl.DeviceIdType.MESH

    def device(slice_number, target):
        target = (target + space) % space
        return {
            "x": slice_number // 2, "core": slice_number % 2, "zh": target // rest, "rest": target % rest,
        }

    crossing = core != zh
    later, earlier = number < tm - 1, number > 0
    barrier = pltpu.get_barrier_semaphore()
    partner = {"core": zh, "zh": core}

    def greet(where):
        pl.semaphore_signal(barrier, inc=1, device_id=where, device_id_type=mesh_type)

    @pl.when(crossing)
    def _():
        greet(partner)

    @pl.when(later)
    def _():
        for shift in (-1, 0, 1):
            greet(device(number + 1, place + shift))

    @pl.when(earlier)
    def _():
        for shift in (-1, 0, 1):
            greet(device(number - 1, place + shift))

    amount = jnp.where(crossing, 1, 0) + jnp.where(later, 3, 0) + jnp.where(earlier, 3, 0)
    pl.semaphore_wait(barrier, amount)

    swap = pltpu.make_async_remote_copy(
        src_ref=jump, dst_ref=landed, send_sem=swap_sems.at[0], recv_sem=swap_sems.at[1],
        device_id=partner, device_id_type=mesh_type,
    )

    @pl.when(crossing)
    def _():
        swap.start()

    def outgoing():
        target = number + 1

        def one(n, source, landing, shift):
            return pltpu.make_async_remote_copy(
                src_ref=source, dst_ref=landing, send_sem=send_sems.at[n], recv_sem=recv_sems.at[n],
                device_id=device(target, place + shift), device_id_type=mesh_type,
            )

        return [
            one(0, out, current.at[:, 8 : 8 + rows, :], 0),
            one(1, edge_out.at[0], edge_in.at[1], -1),
            one(2, edge_out.at[1], edge_in.at[0], 1),
        ]

    @pl.when(crossing)
    def _():
        swap.wait()

    @pl.when(core == zh)
    def _():
        landed[...] = jump[...]

    @pl.when(number == 0)
    def _():
        out[...] = opening[...] + landed[...]

    @pl.when(earlier)
    def _():
        for copy in outgoing():
            copy.wait_recv()
        for c in range(3):
            current[c, 7:8, :] = edge_in[0, c : c + 1, :]
            current[c, 8 + rows : 9 + rows, :] = edge_in[1, c : c + 1, :]
        for at in range(0, rows, 8):
            inside = [current[c, 8 + at : 16 + at, :] for c in range(3)]
            weights = [links[n, at : at + 8, :] for n in range(4)]
            effective = []
            for c in range(3):
                m = inside[c]
                total = weights[0] * (current[c, 7 + at : 15 + at, :] - m)
                total = total + weights[1] * (current[c, 9 + at : 17 + at, :] - m)
                total = total + weights[2] * (pltpu.roll(m, 1, 1) - m)
                total = total + weights[3] * (pltpu.roll(m, grid - 1, 1) - m)
                total = total + field[c, at : at + 8, :]
                effective.append(total - m if c == 2 else total)
            first = cross_of(inside, effective)
            second = cross_of(inside, first)
            for c in range(3):
                value = -(first[c] + damping * second[c]) * (1.0 / (1.0 + damping * damping))
                moved = inside[c] + FINE * step_time * value
                out[c, at : at + 8, :] = moved + landed[c, at : at + 8, :]

    @pl.when(later)
    def _():
        for c in range(3):
            edge_out[0, c : c + 1, :] = out[c, 0:1, :]
            edge_out[1, c : c + 1, :] = out[c, rows - 1 : rows, :]
        copies = outgoing()
        for copy in copies:
            copy.start()
        for copy in copies:
            copy.wait_send()


def sweep(space, tm, jump, opening, field, links):
    _, rows, grid = opening.shape
    f32 = jnp.float32

    def kernel(*refs):
        sweep_kernel(space, tm, *refs)

    return pl.pallas_call(
        kernel,
        out_shape=jax.ShapeDtypeStruct(opening.shape, f32),
        in_specs=[pl.BlockSpec(memory_space=pltpu.VMEM)] * 4,
        out_specs=pl.BlockSpec(memory_space=pltpu.VMEM),
        scratch_shapes=[
            pltpu.VMEM((3, rows + 16, grid), f32),
            pltpu.VMEM((3, rows, grid), f32),
            pltpu.VMEM((2, 8, grid), f32),
            pltpu.VMEM((2, 8, grid), f32),
            pltpu.SemaphoreType.DMA((2,)),
            pltpu.SemaphoreType.DMA((3,)),
            pltpu.SemaphoreType.DMA((3,)),
        ],
        compiler_params=pltpu.CompilerParams(
            collective_id=1, has_side_effects=True, vmem_limit_bytes=32 * 1024 * 1024
        ),
    )(jump, opening, field, links)


def make_shards(tm, space):
    rest = space // 2

    def shards(initial_state, applied_field, coupling):
        rows, _, grid = initial_state.shape
        length = 2 * grid
        width = length // space
        depth = tm
        part = lax.axis_index(RING)
        new_slice = lax.axis_index(("x", "zh"))
        tall, blocks = real_tables(grid, space)

        start = jnp.transpose(initial_state, (1, 0, 2))
        field = jnp.transpose(applied_field, (1, 0, 2))
        pack = jnp.concatenate([start, field, coupling[None]], axis=0)

        def fetch(block, shift):
            pairs = []
            for device in range(2 * space):
                core, zh, r = device // space, device // rest % 2, device % rest
                wanted = core * rest + r + shift
                if 0 <= wanted < space:
                    pairs.append((zh * space + wanted, device))
            return lax.ppermute(block, LOCAL, pairs)

        middle = fetch(pack, 0)
        before = fetch(pack[:, rows - depth :], -1)
        after = fetch(pack[:, :depth], 1)
        wide = jnp.concatenate([before, middle, after], axis=1)
        wide_coupling = wide[6]
        wide_field = wide[3:6]
        state = wide[:3]
        fine_start, coarse_end = state, state
        for n in range(tm):
            stepped = jnp.pad(
                coarse(state, wide_coupling, wide_field[:, 1:-1]), ((0, 0), (1, 1), (0, 0))
            )
            here = new_slice == n
            fine_start = jnp.where(here, state, fine_start)
            coarse_end = jnp.where(here, stepped, coarse_end)
            state = stepped
        fine_field = wide_field[:, depth:-depth]
        fine_coupling = wide_coupling[depth - 1 : rows + depth + 1]
        coarse_end = coarse_end[:, depth:-depth]

        slot = jnp.arange(length, dtype=jnp.int32)
        wave_y = jnp.where(slot == grid, grid, slot % grid)
        lane = jnp.arange(width, dtype=jnp.int32)
        wave_x = part * (width // 2) + lane % (width // 2)
        wave_x = jnp.where((wave_x == 0) & (lane >= width // 2), grid, wave_x)
        txx, tyy, txy, tzz = spectral_tensor(wave_y[:, None], wave_x[None, :], length)
        same = ((slot >= grid)[:, None]) == ((lane >= width // 2)[None, :])
        txy = jnp.where(same, -txy, txy)

        links = links_of(wide_coupling, depth)
        cut = np.transpose(blocks.reshape(grid, space, width), (1, 0, 2))
        tables = [part_ for table in (cut, tall.T, tall, blocks.T) for part_ in halves(table)]
        jump = fine_jump(
            space, fine_start[:, depth:-depth], fine_field, links, coarse_end, jnp.stack([txx, tyy, txy, tzz]), tables
        )
        def beside(block, shift):
            pairs = [(i - shift, i) for i in range(space) if 0 <= i - shift < space]
            return lax.ppermute(block, ("zh", "rest"), pairs)

        packed = jnp.concatenate([start, coupling[None]], axis=0)
        home = jnp.concatenate([beside(packed[:, -1:], 1), packed, beside(packed[:, :1], -1)], axis=1)
        home_coupling = home[3]
        opening = coarse(home[:3], home_coupling, field)
        end = sweep(space, tm, jump, opening, field, links_of(home_coupling, 1))
        return jnp.transpose(end, (1, 0, 2))[None]

    return shards


def solution(mesh):
    tm, space = mesh.shape["tm"], mesh.shape["space"]
    finer = Mesh(mesh.devices.reshape(tm // 2, 2, 2, space // 2), EVERY)
    rows = ("zh", "rest")
    return jax.shard_map(
        make_shards(tm, space),
        mesh=finer,
        in_specs=(P(rows, None, None), P(rows, None, None), P(rows, None)),
        out_specs=P(("x", "core"), rows, None, None),
        check_vma=False,
    )
```

profile of v0, /device:TPU:3, one launch (start us, length us, event | category | flops | bytes accessed | tf_op | source)
XLA Modules:
  0.0 175.6 jit_solution(11683636994242314305)
XLA Ops:
  0.0 1.3 pad_maximum_fusion.2
  1.3 4.8 %collective-permute-start.1 = (f32[7,64,512]{2,1,0:T(8,128)S(1)}, f32[7,64,512]{2,1,0:T(8,128)S(1)}, u32[]{:S(2)}, u32[]{:S(2)}) collective-permute-start(f32[7,64,512]{2,1,0:T(8,128)S(1)} %pad_maximum_fusion.2), channel_id=1, source_target_pairs={{0,0},{1,1},{2,2},{3,3},{8,4},{9,5},{10,6},{11,7},{4,8},{5,9},{6,1... | collective-permute-start | bytes 2752520 | tf_op jit(solution)/shard_map/ppermute | solution.py:515
  6.1 0.7 fusion.94
  6.8 1.3 collective-permute-start.2
  8.1 6.1 %collective-permute-start = (f32[7,4,512]{2,1,0:T(4,128)}, f32[7,4,512]{2,1,0:T(4,128)S(1)}, u32[]{:S(2)}, u32[]{:S(2)}) collective-permute-start(f32[7,4,512]{2,1,0:T(4,128)} %get-tuple-element.38), channel_id=1, source_target_pairs={{0,1},{1,2},{2,3},{8,5},{9,6},{10,7},{3,8},{4,9},{5,10},{6,11},{11... | collective-permute-start | bytes 172040 | tf_op jit(solution)/shard_map/ppermute | solution.py:515
  14.2 4.0 %collective-permute-start.4 = (f32[4,1,512]{2,1,0:T(1,128)S(1)}, f32[4,1,512]{2,1,0:T(1,128)S(1)}, u32[]{:S(2)}, u32[]{:S(2)}) collective-permute-start(f32[4,1,512]{2,1,0:T(1,128)S(1)} %get-tuple-element.43), channel_id=1, source_target_pairs={{0,1},{1,2},{2,3},{3,4},{4,5},{5,6},{6,7},{8,9},{9,10},{10,11},{11... | collective-permute-start | bytes 24584 | tf_op jit(solution)/shard_map/ppermute | solution.py:554
  18.2 1.3 collective-permute-start.3
  19.8 0.8 multiply_multiply_fusion
  20.6 1.5 pad_maximum_fusion.refs_4_
  22.1 0.5 collective-permute-done.3
  23.4 5.8 %collective-permute-done.2 = f32[7,4,512]{2,1,0:T(4,128)S(1)} collective-permute-done((f32[7,4,512]{2,1,0:T(4,128)}, f32[7,4,512]{2,1,0:T(4,128)S(1)}, u32[]{:S(2)}, u32[]{:S(2)}) %collective-permute-start.2) | collective-permute-done | bytes 57376 | tf_op jit(solution)/shard_map/ppermute | solution.py:515
  29.7 0.4 fusion.20
  30.5 0.4 fusion.28
  31.4 0.4 fusion.36
  32.0 0.4 fusion.58
  32.4 0.4 fusion.44
  33.1 0.5 fusion.61
  33.7 1.2 pad_select_fusion
  34.8 0.8 slice.464.refs_1_
  35.6 0.9 fusion.11.refs_2_
  36.5 109.2 %shard_map.109.refs_0_ = f32[3,64,512]{2,1,0:T(8,128)} custom-call(f32[3,64,512]{2,1,0:T(8,128)} %get-tuple-element.31.refs_0_, f32[3,64,512]{2,1,0:T(8,128)} %slice.464.refs_1_, f32[4,64,512]{2,1,0:T(8,128)} %fusion.11.refs_2_, f32[3,64,512]{2,1,0:T(8,128)} %get-tuple-element.30.refs_3_, f32[4,1024,128]{2,1,0:T(8,128)} %pad_maximum_fusion.refs_4_, ...), custom_call_target="tpu_custom_call" | custom-call | tf_op jit(solution)/shard_map/pallas_call | solution.py:302
  145.7 1.0 copy-done.1
  146.7 28.1 %shard_map.110 = f32[3,64,512]{2,1,0:T(8,128)S(1)} custom-call(f32[3,64,512]{2,1,0:T(8,128)S(1)} %copy-done.1, f32[3,64,512]{2,1,0:T(8,128)S(1)} %fusion.77.refs_1_, f32[3,64,512]{2,1,0:T(8,128)S(1)} %bitcast.31, f32[4,64,512]{2,1,0:T(8,128)S(1)} %maximum_multiply_fusion.refs_3_), custom_call_target="tpu_custom_call" | custom-call | tf_op jit(solution)/shard_map/pallas_call | solution.py:472
  174.9 0.7 copy.13
  (46 shorter events, 2.9 us)
Async XLA Ops:
  0.0 14.1 %copy-start.3 = (f32[64,512]{1,0:T(8,128)S(1)}, f32[64,512]{1,0:T(8,128)}, u32[]{:S(2)}) copy-start(f32[64,512]{1,0:T(8,128)} %param.13) | copy-start | bytes 393220
  0.0 14.1 %copy-start.2 = (f32[64,3,512]{2,0,1:T(8,128)S(1)}, f32[64,3,512]{2,0,1:T(8,128)}, u32[]{:S(2)}) copy-start(f32[64,3,512]{2,0,1:T(8,128)} %param.11) | copy-start | bytes 1179652
  1.3 27.9 %collective-permute-start.1 = (f32[7,64,512]{2,1,0:T(8,128)S(1)}, f32[7,64,512]{2,1,0:T(8,128)S(1)}, u32[]{:S(2)}, u32[]{:S(2)}) collective-permute-start(f32[7,64,512]{2,1,0:T(8,128)S(1)} %pad_maximum_fusion.2), channel_id=1, source_target_pairs={{0,0},{1,1},{2,2},{3,3},{8,4},{9,5},{10,6},{11,7},{4,8},{5,9},{6,1... | collective-permute-start | bytes 2752520 | tf_op jit(solution)/shard_map/ppermute | solution.py:515
  6.8 22.4 %collective-permute-start.2 = (f32[7,4,512]{2,1,0:T(4,128)}, f32[7,4,512]{2,1,0:T(4,128)S(1)}, u32[]{:S(2)}, u32[]{:S(2)}) collective-permute-start(f32[7,4,512]{2,1,0:T(4,128)} %get-tuple-element.39), channel_id=1, source_target_pairs={{1,0},{2,1},{3,2},{4,3},{9,4},{10,5},{11,6},{12,7},{5,8},{6,9},{7,... | collective-permute-start | bytes 172040 | tf_op jit(solution)/shard_map/ppermute | solution.py:515
  8.1 21.1 %collective-permute-start = (f32[7,4,512]{2,1,0:T(4,128)}, f32[7,4,512]{2,1,0:T(4,128)S(1)}, u32[]{:S(2)}, u32[]{:S(2)}) collective-permute-start(f32[7,4,512]{2,1,0:T(4,128)} %get-tuple-element.38), channel_id=1, source_target_pairs={{0,1},{1,2},{2,3},{8,5},{9,6},{10,7},{3,8},{4,9},{5,10},{6,11},{11... | collective-permute-start | bytes 172040 | tf_op jit(solution)/shard_map/ppermute | solution.py:515
  14.2 7.9 %collective-permute-start.4 = (f32[4,1,512]{2,1,0:T(1,128)S(1)}, f32[4,1,512]{2,1,0:T(1,128)S(1)}, u32[]{:S(2)}, u32[]{:S(2)}) collective-permute-start(f32[4,1,512]{2,1,0:T(1,128)S(1)} %get-tuple-element.43), channel_id=1, source_target_pairs={{0,1},{1,2},{2,3},{3,4},{4,5},{5,6},{6,7},{8,9},{9,10},{10,11},{11... | collective-permute-start | bytes 24584 | tf_op jit(solution)/shard_map/ppermute | solution.py:554
  18.2 4.4 %collective-permute-start.3 = (f32[4,1,512]{2,1,0:T(1,128)S(1)}, f32[4,1,512]{2,1,0:T(1,128)S(1)}, u32[]{:S(2)}, u32[]{:S(2)}) collective-permute-start(f32[4,1,512]{2,1,0:T(1,128)S(1)} %get-tuple-element.42), channel_id=1, source_target_pairs={{1,0},{2,1},{3,2},{4,3},{5,4},{6,5},{7,6},{9,8},{10,9},{11,10},{12... | collective-permute-start | bytes 24584 | tf_op jit(solution)/shard_map/ppermute | solution.py:554
  20.6 2.1 %copy-start = (f32[64,3,512]{2,0,1:T(8,128)S(1)}, f32[64,3,512]{2,0,1:T(8,128)}, u32[]{:S(2)}) copy-start(f32[64,3,512]{2,0,1:T(8,128)} %param.12) | copy-start | bytes 1179652
  145.7 1.0 copy-start.1
where the time goes:
time: 176 us
  Pallas kernels  137 us (78%)
  starting transfers between devices  17.5 us (10%)
  other arithmetic  10.6 us (6%)
  waiting for transfers between devices  6.33 us (4%)
  local copies, waits for them, and re-layouts  3.52 us (2%)
    pallas_call x1, Pallas kernels, fine_jump(): pl.pallas_call(kernel, out_shape=jax.ShapeDtypeStruct(start.shape, f32),...  109 us
    pallas_call x1, Pallas kernels, sweep(): pl.pallas_call(kernel, out_shape=jax.ShapeDtypeStruct(opening.shape, f32)...  28.1 us
    ppermute x3, starting transfers between devices, fetch(): return lax.ppermute(block, LOCAL, pairs)  12.1 us
    ppermute x3, waiting for transfers between devices, fetch(): return lax.ppermute(block, LOCAL, pairs)  5.81 us
    ppermute x2, starting transfers between devices, beside(): return lax.ppermute(block, ('zh', 'rest'), pairs)  5.33 us
  transfers between devices with their start and end apart: 5, of which 2 were waited for; matrix products, arithmetic and copies ran while one was open for 2% of the time, Pallas kernels for 0%

commit v1 on v0

v1 whole, which is shorter than its diff:
```python
import functools
import math

import jax
import jax.numpy as jnp
import numpy as np
from jax import lax
from jax.experimental import pallas as pl
from jax.experimental.pallas import tpu as pltpu
from jax.sharding import Mesh, PartitionSpec as P

FINE = 2
step_time = 0.06
damping = 0.02
stiffness = 0.25
thickness = 8.0
PASSES = 3

EVERY = ("x", "core", "zh", "rest")


def sector_tables(grid):
    half = grid // 2
    place = 2 * np.arange(half) - (grid - 1)
    wave = np.arange(grid)
    odd_wave = np.where(wave == 0, grid, wave)
    turn = 4 * grid

    def angle(k):
        return 2.0 * np.pi / turn * ((place[:, None] * k[None, :]) % turn)

    table = np.stack([np.cos(angle(wave)), np.sin(angle(odd_wave))]).astype(np.float32)
    fold = np.zeros((grid, grid), np.float32)
    for i in range(half):
        fold[i, i] = fold[grid - 1 - i, i] = fold[i, half + i] = 1.0
        fold[grid - 1 - i, half + i] = -1.0
    return table, fold


def exchange_field(padded, pad_coupling):
    center = padded[:, 1:-1]
    coupling = pad_coupling[1:-1]
    wide = jnp.pad(padded[:, 1:-1], ((0, 0), (0, 0), (1, 1)))
    wide_coupling = jnp.pad(coupling, ((0, 0), (1, 1)))
    total = pad_coupling[2:] * (padded[:, 2:] - center)
    total = total + pad_coupling[:-2] * (padded[:, :-2] - center)
    total = total + wide_coupling[:, 2:] * (wide[:, :, 2:] - center)
    total = total + wide_coupling[:, :-2] * (wide[:, :, :-2] - center)
    return stiffness * coupling * total


def cross(a, b):
    return jnp.stack([a[1] * b[2] - a[2] * b[1], a[2] * b[0] - a[0] * b[2], a[0] * b[1] - a[1] * b[0]])


def torque(magnet, effective):
    first = cross(magnet, effective)
    return -(first + damping * cross(magnet, first)) * (1.0 / (1.0 + damping * damping))


def coarse(padded, pad_coupling, field):
    center = padded[:, 1:-1]
    effective = exchange_field(padded, pad_coupling) + field
    effective = jnp.stack([effective[0], effective[1], effective[2] - center[2]])
    return center + FINE * step_time * torque(center, effective)


def halves(table):
    high = table.astype(jnp.bfloat16)
    return [high, (table - high.astype(np.float32)).astype(jnp.bfloat16)]


def split(value):
    high = value.astype(jnp.bfloat16)
    return high, (value - high.astype(jnp.float32)).astype(jnp.bfloat16)


def dot3(left_high, left_low, right_high, right_low):
    def one(a, b):
        return jnp.dot(a, b, preferred_element_type=jnp.float32)

    return one(left_high, right_high) + (one(left_high, right_low) + one(left_low, right_high))


def cross_of(a, b):
    return [a[1] * b[2] - a[2] * b[1], a[2] * b[0] - a[0] * b[2], a[0] * b[1] - a[1] * b[0]]


def product(passes, left, right):
    def one(a, b):
        return jnp.dot(a, b, preferred_element_type=jnp.float32)

    value = one(left[0], right[0])
    if passes > 1:
        value = value + one(left[1], right[0])
    if passes > 2:
        value = value + one(left[0], right[1])
    return value


def put(passes, pair, where, value):
    high, low = split(value)
    pair[0][where] = high
    if passes > 1:
        pair[1][where] = low


def fine_kernel(
    space,
    mine, theirs, field, coupling,
    table_high, table_low, turned_high, turned_low, fold, unfold,
    out,
    current, rate, base, probe, demag, far_start, far_field, far_coupling, links, tensors,
    edge_out, edge_in, wide_high, wide_low, send_xy, send_z, land, back, got_xy, got_z,
    plane_high, plane_low, mixed_high, mixed_low,
    swap_sems, edge_sems, send_sems, land_sems, back_sems, got_sems,
):
    _, strip, grid = mine.shape
    rest_count = space // 2
    half = grid // 2
    multi = rest_count // 4
    width = grid // multi
    core, zh, rest = lax.axis_index("core"), lax.axis_index("zh"), lax.axis_index("rest")
    order = jnp.where(zh == 0, rest, rest_count - 1 - rest)
    number = 2 * order + core
    unit = rest // multi
    share = rest % multi
    row_odd, column_odd = unit // 2, unit % 2

    def at_place(core_index, rest_index):
        return {"core": core_index, "rest": rest_index}

    def owner(index):
        place = index // 2
        return at_place(index % 2, jnp.where(zh == 0, place, rest_count - 1 - place))

    def remote(source, target, send_sem, recv_sem, where):
        return pltpu.make_async_remote_copy(
            src_ref=source, dst_ref=target, send_sem=send_sem, recv_sem=recv_sem,
            device_id=where, device_id_type=pl.DeviceIdType.MESH,
        )

    barrier = pltpu.get_barrier_semaphore()
    partner = {"zh": 1 - zh, "rest": rest_count - 1 - rest}

    def greet(k, carry):
        pl.semaphore_signal(
            barrier, inc=1, device_id=owner((number + k) % space), device_id_type=pl.DeviceIdType.MESH
        )
        return carry

    lax.fori_loop(1, space, greet, 0)
    pl.semaphore_signal(barrier, inc=1, device_id=partner, device_id_type=pl.DeviceIdType.MESH)
    pl.semaphore_wait(barrier, space)

    swaps = [
        remote(source, target, swap_sems.at[0, n], swap_sems.at[1, n], partner)
        for n, (source, target) in enumerate(
            ((theirs, far_start), (field, far_field), (coupling, far_coupling))
        )
    ]
    for swap in swaps:
        swap.start()

    def fill(i, carry):
        at = pl.multiple_of(i * 64, 64)
        slot_rows = at + lax.broadcasted_iota(jnp.int32, (64, width), 0)
        slot_columns = share * width + lax.broadcasted_iota(jnp.int32, (64, width), 1)
        unit_length = 2.0 * math.pi / (2 * grid)

        def parts(odd_rows, odd_columns):
            rows = jnp.where((slot_rows == 0) & (odd_rows == 1), grid, slot_rows)
            columns = jnp.where((slot_columns == 0) & (odd_columns == 1), grid, slot_columns)
            wave_rows = unit_length * rows.astype(jnp.float32)
            wave_columns = unit_length * columns.astype(jnp.float32)
            squared = wave_rows * wave_rows + wave_columns * wave_columns
            nonzero = squared > 0.0
            safe = jnp.where(nonzero, squared, 1.0)
            scaled = jnp.sqrt(safe) * thickness
            film = jnp.where(nonzero, (1.0 - jnp.exp(-scaled)) / scaled, 1.0)
            weight = jnp.where(slot_rows == 0, 1.0, 2.0) * jnp.where(slot_columns == 0, 1.0, 2.0)
            weight = weight * (-1.0 / (4 * grid * grid))
            return wave_rows, wave_columns, film, (1.0 - film) / safe, weight

        @pl.when(core == 1)
        def _():
            wave_rows, wave_columns, _, in_plane, weight = parts(row_odd, column_odd)
            tensors[0, pl.ds(at, 64), :] = in_plane * wave_columns * wave_columns * weight
            mixed = in_plane * wave_columns * wave_rows * weight
            sign = jnp.where((row_odd == column_odd) == (zh == 0), -1.0, 1.0)
            tensors[2, pl.ds(at, 64), :] = jnp.where((slot_rows == 0) | (slot_columns == 0), 0.0, mixed * sign)
            wave_rows, wave_columns, _, in_plane, weight = parts(1 - row_odd, 1 - column_odd)
            tensors[1, pl.ds(at, 64), :] = in_plane * wave_rows * wave_rows * weight

        @pl.when(core == 0)
        def _():
            _, _, film, _, weight = parts(row_odd, column_odd)
            tensors[0, pl.ds(at, 64), :] = film * weight

        return carry

    lax.fori_loop(0, grid // 64, fill, 0)

    def make_links(t, source):
        own = source[8 : 8 + strip, :]
        lane = lax.broadcasted_iota(jnp.int32, (strip, grid), 1)
        links[t, 0] = stiffness * own * source[7 : 7 + strip, :]
        links[t, 1] = stiffness * own * source[9 : 9 + strip, :]
        links[t, 2] = jnp.where(lane == 0, 0.0, stiffness * own * pltpu.roll(own, 1, 1))
        links[t, 3] = jnp.where(lane == grid - 1, 0.0, stiffness * own * pltpu.roll(own, grid - 1, 1))

    make_links(0, coupling)
    base[0] = mine[...]
    swaps[0].wait()
    base[1] = far_start[...]
    current[:, :, 8 : 8 + strip, :] = base[...]
    probe[...] = base[...]

    def to_unit(kind, r):
        target = (rest + r) % rest_count
        if kind == 1:
            source, landing = send_xy.at[target // multi], land.at[:, pl.ds(number * strip, strip), :]
        else:
            source, landing = send_z.at[target // multi], land.at[0, pl.ds(number * strip, strip), :]
        return remote(source, landing, send_sems.at[kind, r], land_sems.at[number], at_place(kind, target))

    def landed(kind, index):
        if kind == 1:
            source, landing = send_xy.at[0], land.at[:, pl.ds(index * strip, strip), :]
        else:
            source, landing = send_z.at[0], land.at[0, pl.ds(index * strip, strip), :]
        return remote(source, landing, send_sems.at[kind, 0], land_sems.at[index], owner(index))

    def to_owner(kind, k):
        index = (number + k) % space
        if kind == 1:
            source, landing = back.at[:, pl.ds(index * strip, strip), :], got_xy.at[rest]
        else:
            source, landing = back.at[0, pl.ds(index * strip, strip), :], got_z.at[rest]
        return remote(source, landing, back_sems.at[k], got_sems.at[kind, rest], owner(index))

    def gotten(kind, r):
        if kind == 1:
            source, landing = back.at[:, pl.ds(0, strip), :], got_xy.at[r]
        else:
            source, landing = back.at[0, pl.ds(0, strip), :], got_z.at[r]
        return remote(source, landing, back_sems.at[0], got_sems.at[kind, r], at_place(kind, r))

    def transform(kind, passes):
        planes = [(row_odd, column_odd), (1 - row_odd, 1 - column_odd)] if kind == 1 else [(row_odd, column_odd)]
        columns = pl.ds(pl.multiple_of(share * width, width), width)
        for n, (_, odd) in enumerate(planes):
            spectrum = product(
                passes, split(land[n]), (table_high[odd, :, columns], table_low[odd, :, columns])
            )
            put(passes, (plane_high, plane_low), n, spectrum)
        step = half

        def mix(i, carry):
            at = pl.multiple_of(i * step, step)
            lines = pl.ds(at, step)
            both = [
                product(
                    passes, (turned_high[odd, lines, :], turned_low[odd, lines, :]), (plane_high[n], plane_low[n])
                )
                for n, (odd, _) in enumerate(planes)
            ]
            if kind == 1:
                cross_term = tensors[2, lines, :]
                values = [
                    tensors[0, lines, :] * both[0] + cross_term * both[1],
                    cross_term * both[0] + tensors[1, lines, :] * both[1],
                ]
            else:
                values = [tensors[0, lines, :] * both[0]]
            for n, value in enumerate(values):
                put(passes, (mixed_high, mixed_low), (n, lines), value)
            return carry

        lax.fori_loop(0, grid // step, mix, 0)
        for n, (odd_rows, odd_columns) in enumerate(planes):
            film = product(
                passes, (table_high[odd_rows], table_low[odd_rows]), (mixed_high[n], mixed_low[n])
            )
            back[n] = product(
                passes, split(film), (turned_high[odd_columns, columns, :], turned_low[odd_columns, columns, :])
            )

    def unit_work(kind, passes):
        @pl.when(core == kind)
        def _():
            def take(k, carry):
                landed(kind, (number + k) % space).wait_recv()
                return carry

            lax.fori_loop(1, space, take, 0)
            transform(kind, passes)

            def push(k, carry):
                to_owner(kind, k).start()
                return carry

            lax.fori_loop(1, space, push, 0)
            own = pl.ds(pl.multiple_of(number * strip, strip), strip)
            if kind == 1:
                got_xy[rest] = back[:, own, :]
            else:
                got_z[rest] = back[0, own, :]

    def unit_end(kind):
        @pl.when(core == kind)
        def _():
            def drain(k, carry):
                to_owner(kind, k).wait_send()
                return carry

            lax.fori_loop(1, space, drain, 0)

    def evaluate(parity, passes, first):
        for t in range(2):
            for c in range(3):
                edge_out[0, 3 * t + c : 3 * t + c + 1, :] = current[t, c, 8:9, :]
                edge_out[1, 3 * t + c : 3 * t + c + 1, :] = current[t, c, 7 + strip : 8 + strip, :]
        outward = remote(
            edge_out.at[0], edge_in.at[parity, 1], edge_sems.at[parity, 0], edge_sems.at[parity, 1], owner((number + space - 1) % space)
        )
        inward = remote(
            edge_out.at[1], edge_in.at[parity, 0], edge_sems.at[parity, 2], edge_sems.at[parity, 3], owner((number + 1) % space)
        )
        fold_passes = min(passes, 2)
        for c in range(3):
            near, far = probe[0, c], probe[1, c]
            for p, value in enumerate((near + far, near - far)):
                put(fold_passes, (wide_high, wide_low), pl.ds((3 * p + c) * strip, strip), value)
        folded = product(fold_passes, (wide_high[...], wide_low[...]), (fold[...],))
        for p in range(2):
            for q in range(2):
                for c in range(3):
                    piece = folded[(3 * p + c) * strip : (3 * p + c + 1) * strip, q * half : (q + 1) * half]
                    if c == 0:
                        send_xy[2 * p + q, 0] = piece
                    elif c == 1:
                        send_xy[2 * (1 - p) + 1 - q, 1] = piece
                    else:
                        send_z[2 * p + q] = piece

        def launch(r, carry):
            for kind in range(2):
                @pl.when((core != kind) | (r != 0))
                def _(kind=kind):
                    to_unit(kind, r).start()

            return carry

        lax.fori_loop(0, rest_count, launch, 0)
        outward.start()
        inward.start()
        own = pl.ds(pl.multiple_of(number * strip, strip), strip)

        @pl.when(core == 1)
        def _():
            land[:, own, :] = send_xy[unit]

        @pl.when(core == 0)
        def _():
            land[0, own, :] = send_z[unit]

        unit_work(1, passes)
        unit_work(0, passes)

        def settle(r, carry):
            for kind in range(2):
                @pl.when((core != kind) | (r != 0))
                def _(kind=kind):
                    to_unit(kind, r).wait_send()
                    gotten(kind, (rest + r) % rest_count).wait_recv()

            return carry

        lax.fori_loop(0, rest_count, settle, 0)
        outward.wait()
        inward.wait()
        for p in range(2):
            for q in range(2):
                for c in range(3):
                    source = 2 * (1 - p) + 1 - q if c == 1 else 2 * p + q
                    value = None
                    for k in range(multi):
                        piece = got_z[source * multi + k] if c == 2 else got_xy[source * multi + k, c]
                        value = piece if value is None else value + piece
                    where = (pl.ds((3 * p + c) * strip, strip), pl.ds(q * half, half))
                    put(fold_passes, (wide_high, wide_low), where, value)
        unfolded = product(fold_passes, (wide_high[...], wide_low[...]), (unfold[...],))
        for c in range(3):
            even = unfolded[c * strip : (c + 1) * strip]
            odd = unfolded[(3 + c) * strip : (4 + c) * strip]
            for t, value in enumerate((even + odd, even - odd)):
                if first:
                    demag[0, t, c] = value
                    demag[1, t, c] = value
                elif parity == 0:
                    moved = demag[0, t, c] + value
                    demag[0, t, c] = moved
                    demag[1, t, c] = moved
                else:
                    demag[1, t, c] = demag[0, t, c] + value
        if first:
            for swap in swaps[1:]:
                swap.wait()
            make_links(1, far_coupling)
        unit_end(1)
        unit_end(0)
        last = number == space - 1
        for t in range(2):
            for c in range(3):
                current[t, c, 7:8, :] = edge_in[parity, 0, 3 * t + c : 3 * t + c + 1, :]
                facing = current[1 - t, c, 7 + strip : 8 + strip, :]
                arrived = edge_in[parity, 1, 3 * t + c : 3 * t + c + 1, :]
                current[t, c, 8 + strip : 9 + strip, :] = jnp.where(last, facing, arrived)
        for t in range(2):
            applied = (field, far_field)[t]
            for at in range(0, strip, 8):
                rows = slice(at, at + 8)
                inside = [current[t, c, 8 + at : 16 + at, :] for c in range(3)]
                weights = [links[t, n, rows, :] for n in range(4)]
                effective = []
                for c in range(3):
                    m = inside[c]
                    total = weights[0] * (current[t, c, 7 + at : 15 + at, :] - m)
                    total = total + weights[1] * (current[t, c, 9 + at : 17 + at, :] - m)
                    total = total + weights[2] * (pltpu.roll(m, 1, 1) - m)
                    total = total + weights[3] * (pltpu.roll(m, grid - 1, 1) - m)
                    effective.append(total + demag[1, t, c, rows, :] + applied[c, rows, :])
                turned = cross_of(inside, effective)
                again = cross_of(inside, turned)
                for c in range(3):
                    value = -(turned[c] + damping * again[c]) * (1.0 / (1.0 + damping * damping))
                    if parity == 0:
                        rate[t, c, rows, :] = value
                        probe[t, c, rows, :] = step_time * value
                    else:
                        moved = 0.5 * step_time * (rate[t, c, rows, :] + value)
                        probe[t, c, rows, :] = moved
                        base[t, c, rows, :] = base[t, c, rows, :] + moved
        if parity == 0:
            current[:, :, 8 : 8 + strip, :] = base[...] + probe[...]
        else:
            current[:, :, 8 : 8 + strip, :] = base[...]

    evaluate(0, 3, True)

    def fine_step(i, carry):
        evaluate(1, PASSES, False)
        evaluate(0, PASSES, False)
        return carry

    lax.fori_loop(1, FINE, fine_step, 0)
    evaluate(1, PASSES, False)
    out[...] = base[...]


def fine_states(space, mine, theirs, field, coupling, tables):
    _, strip, grid = mine.shape
    half = grid // 2
    rest_count = space // 2
    width = grid * 4 // rest_count
    f32, bf16 = jnp.float32, jnp.bfloat16
    operands = [mine, theirs, field, coupling, *tables]
    return pl.pallas_call(
        functools.partial(fine_kernel, space),
        out_shape=jax.ShapeDtypeStruct((2, 3, strip, grid), f32),
        in_specs=[pl.BlockSpec(memory_space=pltpu.VMEM)] * len(operands),
        out_specs=pl.BlockSpec(memory_space=pltpu.VMEM),
        scratch_shapes=[
            pltpu.VMEM((2, 3, strip + 16, grid), f32),
            pltpu.VMEM((2, 3, strip, grid), f32),
            pltpu.VMEM((2, 3, strip, grid), f32),
            pltpu.VMEM((2, 3, strip, grid), f32),
            pltpu.VMEM((2, 2, 3, strip, grid), f32),
            pltpu.VMEM((3, strip, grid), f32),
            pltpu.VMEM((3, strip, grid), f32),
            pltpu.VMEM((strip + 16, grid), f32),
            pltpu.VMEM((2, 4, strip, grid), f32),
            pltpu.VMEM((3, grid, width), f32),
            pltpu.VMEM((2, 8, grid), f32),
            pltpu.VMEM((2, 2, 8, grid), f32),
            pltpu.VMEM((6 * strip, grid), bf16),
            pltpu.VMEM((6 * strip, grid), bf16),
            pltpu.VMEM((4, 2, strip, half), f32),
            pltpu.VMEM((4, strip, half), f32),
            pltpu.VMEM((2, half, half), f32),
            pltpu.VMEM((2, half, half), f32),
            pltpu.VMEM((rest_count, 2, strip, half), f32),
            pltpu.VMEM((rest_count, strip, half), f32),
            pltpu.VMEM((2, half, width), bf16),
            pltpu.VMEM((2, half, width), bf16),
            pltpu.VMEM((2, grid, width), bf16),
            pltpu.VMEM((2, grid, width), bf16),
            pltpu.SemaphoreType.DMA((2, 3)),
            pltpu.SemaphoreType.DMA((2, 4)),
            pltpu.SemaphoreType.DMA((2, rest_count)),
            pltpu.SemaphoreType.DMA((space,)),
            pltpu.SemaphoreType.DMA((space,)),
            pltpu.SemaphoreType.DMA((2, rest_count)),
        ],
        compiler_params=pltpu.CompilerParams(
            collective_id=0, has_side_effects=True, vmem_limit_bytes=56 * 1024 * 1024
        ),
    )(*operands)


def sweep_kernel(
    space, tm, fine, coarse_end, field, links, out,
    current, landed, edge_out, edge_in, jump_sends, jump_recvs, send_sems, recv_sems,
):
    _, rows, grid = coarse_end.shape
    strip = rows // 2
    rest_count = space // 2
    core, zh, rest = lax.axis_index("core"), lax.axis_index("zh"), lax.axis_index("rest")
    number = lax.axis_index("x") * 2 + core
    place = zh * rest_count + rest
    order = jnp.where(zh == 0, rest, rest_count - 1 - rest)
    mesh_type = pl.DeviceIdType.MESH
    outward = jnp.where(zh == 0, place + space - 1, place + 1) % space
    inward = jnp.where(zh == 0, place + 1, place + space - 1) % space

    def device(slice_number, target):
        return {
            "x": slice_number // 2, "core": slice_number % 2, "zh": target // rest_count, "rest": target % rest_count,
        }

    native = core == zh
    later, earlier = number < tm - 1, number > 0
    barrier = pltpu.get_barrier_semaphore()
    away = {"core": zh, "zh": 1 - zh, "rest": rest_count - 1 - rest}
    beside = {"core": 1 - core}

    def greet(where):
        pl.semaphore_signal(barrier, inc=1, device_id=where, device_id_type=mesh_type)

    for k in range(2):
        greet({"core": k, "zh": 1 - zh, "rest": rest_count - 1 - rest})
    greet(beside)

    @pl.when(later)
    def _():
        for target in (outward, place, inward):
            greet(device(number + 1, target))

    @pl.when(earlier)
    def _():
        for target in (outward, place, inward):
            greet(device(number - 1, target))

    pl.semaphore_wait(barrier, 3 + jnp.where(later, 3, 0) + jnp.where(earlier, 3, 0))

    def carry_jump(source, n, where):
        return pltpu.make_async_remote_copy(
            src_ref=source, dst_ref=landed.at[core], send_sem=jump_sends.at[n], recv_sem=jump_recvs.at[core],
            device_id=where, device_id_type=mesh_type,
        )

    def await_jump(part):
        pltpu.make_async_remote_copy(
            src_ref=fine.at[0], dst_ref=landed.at[part], send_sem=jump_sends.at[0], recv_sem=jump_recvs.at[part],
            device_id=away, device_id_type=mesh_type,
        ).wait_recv()

    far = carry_jump(fine.at[1], 1, away)
    near = carry_jump(fine.at[0], 0, beside)
    far.start()

    @pl.when(core != zh)
    def _():
        near.start()

    @pl.when(native)
    def _():
        landed[core] = fine[0]
        await_jump(1 - core)

    @pl.when(core != zh)
    def _():
        await_jump(0)
        await_jump(1)

    def outgoing():
        target = number + 1

        def one(n, source, landing, sem, where):
            return pltpu.make_async_remote_copy(
                src_ref=source, dst_ref=landing, send_sem=send_sems.at[n], recv_sem=recv_sems.at[sem],
                device_id=device(target, where), device_id_type=mesh_type,
            )

        outer = jnp.where(order == 0, 0, 1)
        inner = jnp.where(order == rest_count - 1, 1, 0)
        return [
            one(0, out, current.at[:, 8 : 8 + rows, :], 2, place),
            one(1, edge_out.at[0], edge_in.at[outer], outer, outward),
            one(2, edge_out.at[1], edge_in.at[inner], inner, inward),
        ]

    def arrivals():
        def one(source, landing, sem):
            return pltpu.make_async_remote_copy(
                src_ref=source, dst_ref=landing, send_sem=send_sems.at[0], recv_sem=recv_sems.at[sem],
                device_id=device(number - 1, place), device_id_type=mesh_type,
            )

        return [
            one(out, current.at[:, 8 : 8 + rows, :], 2),
            one(edge_out.at[0], edge_in.at[0], 0),
            one(edge_out.at[1], edge_in.at[1], 1),
        ]

    @pl.when(number == 0)
    def _():
        for c in range(3):
            for k in range(2):
                out[c, k * strip : (k + 1) * strip, :] = landed[k, c]

    @pl.when(earlier)
    def _():
        for copy in arrivals():
            copy.wait_recv()
        for c in range(3):
            current[c, 7:8, :] = edge_in[0, c : c + 1, :]
            current[c, 8 + rows : 9 + rows, :] = edge_in[1, c : c + 1, :]
        for at in range(0, rows, 8):
            inside = [current[c, 8 + at : 16 + at, :] for c in range(3)]
            weights = [links[n, at : at + 8, :] for n in range(4)]
            effective = []
            for c in range(3):
                m = inside[c]
                total = weights[0] * (current[c, 7 + at : 15 + at, :] - m)
                total = total + weights[1] * (current[c, 9 + at : 17 + at, :] - m)
                total = total + weights[2] * (pltpu.roll(m, 1, 1) - m)
                total = total + weights[3] * (pltpu.roll(m, grid - 1, 1) - m)
                total = total + field[c, at : at + 8, :]
                effective.append(total - m if c == 2 else total)
            first = cross_of(inside, effective)
            second = cross_of(inside, first)
            k, inner = at // strip, at % strip
            for c in range(3):
                value = -(first[c] + damping * second[c]) * (1.0 / (1.0 + damping * damping))
                moved = inside[c] + FINE * step_time * value
                jump = landed[k, c, inner : inner + 8, :] - coarse_end[c, at : at + 8, :]
                out[c, at : at + 8, :] = moved + jump

    @pl.when(later)
    def _():
        for c in range(3):
            edge_out[0, c : c + 1, :] = out[c, 0:1, :]
            edge_out[1, c : c + 1, :] = out[c, rows - 1 : rows, :]
        copies = outgoing()
        for copy in copies:
            copy.start()
        for copy in copies:
            copy.wait_send()

    far.wait_send()

    @pl.when(core != zh)
    def _():
        near.wait_send()


def sweep(space, tm, fine, coarse_end, field, links):
    _, rows, grid = coarse_end.shape
    f32 = jnp.float32

    def kernel(*refs):
        sweep_kernel(space, tm, *refs)

    return pl.pallas_call(
        kernel,
        out_shape=jax.ShapeDtypeStruct(coarse_end.shape, f32),
        in_specs=[pl.BlockSpec(memory_space=pltpu.VMEM)] * 4,
        out_specs=pl.BlockSpec(memory_space=pltpu.VMEM),
        scratch_shapes=[
            pltpu.VMEM((3, rows + 16, grid), f32),
            pltpu.VMEM((2, 3, rows // 2, grid), f32),
            pltpu.VMEM((2, 8, grid), f32),
            pltpu.VMEM((2, 8, grid), f32),
            pltpu.SemaphoreType.DMA((2,)),
            pltpu.SemaphoreType.DMA((2,)),
            pltpu.SemaphoreType.DMA((3,)),
            pltpu.SemaphoreType.DMA((3,)),
        ],
        compiler_params=pltpu.CompilerParams(
            collective_id=1, has_side_effects=True, vmem_limit_bytes=32 * 1024 * 1024
        ),
    )(fine, coarse_end, field, links)


def links_of(pad_coupling, depth):
    rows = pad_coupling.shape[0] - 2 * depth
    own = pad_coupling[depth : rows + depth]
    flat = jnp.pad(own, ((0, 0), (1, 1)))
    around = [
        pad_coupling[depth - 1 : rows + depth - 1],
        pad_coupling[depth + 1 : rows + depth + 1],
        flat[:, :-2],
        flat[:, 2:],
    ]
    return stiffness * own[None] * jnp.stack(around)


def make_shards(tm, space):
    rest_count = space // 2

    def shards(initial_state, applied_field, coupling):
        rows, _, grid = initial_state.shape
        strip = rows // 2
        depth = tm
        x, core, zh = lax.axis_index("x"), lax.axis_index("core"), lax.axis_index("zh")
        table, fold = sector_tables(grid)

        def inward_order(block):
            return jnp.where(zh == 1, block[::-1], block)

        start = jnp.transpose(inward_order(initial_state), (1, 0, 2))
        field = jnp.transpose(inward_order(applied_field), (1, 0, 2))
        pack = jnp.concatenate([start, field, inward_order(coupling)[None]], axis=0)

        def shift(block, pairs):
            return lax.ppermute(block, ("zh", "rest"), pairs)

        ring = range(1, rest_count)
        before = shift(
            pack[:, rows - depth :], [(i - 1, i) for i in ring] + [(space - i, space - 1 - i) for i in ring]
        )
        after = shift(pack[:, :depth], [(i, i - 1) for i in ring] + [(space - 1 - i, space - i) for i in ring])
        facing = shift(pack[:, rows - depth :], [(rest_count - 1, rest_count), (rest_count, rest_count - 1)])
        place = zh * rest_count + lax.axis_index("rest")
        center = (place == rest_count - 1) | (place == rest_count)
        after = jnp.where(center, facing[:, ::-1], after)
        wide = jnp.concatenate([before, pack, after], axis=1)
        wide_coupling = wide[6]
        wide_field = wide[3:6]
        state = wide[:3]
        mine = theirs = coarse_end = state
        for n in range(tm):
            stepped = jnp.pad(coarse(state, wide_coupling, wide_field[:, 1:-1]), ((0, 0), (1, 1), (0, 0)))
            mine = jnp.where(2 * x + zh == n, state, mine)
            theirs = jnp.where(2 * x + 1 - zh == n, state, theirs)
            coarse_end = jnp.where(2 * x + core == n, stepped, coarse_end)
            state = stepped

        def half_of(block, margin):
            low = block[..., depth - margin : depth + strip + margin, :]
            high = block[..., depth + strip - margin : depth + rows + margin, :]
            return jnp.where(core == 0, low, high)

        tables = [*halves(table), *halves(np.ascontiguousarray(np.transpose(table, (0, 2, 1))))]
        tables += [fold.astype(jnp.bfloat16), np.ascontiguousarray(fold.T).astype(jnp.bfloat16)]
        fine = fine_states(
            space, half_of(mine, 0), half_of(theirs, 0), half_of(wide_field, 0),
            jnp.pad(half_of(wide_coupling, 1), ((7, 7), (0, 0))), tables,
        )
        end = sweep(space, tm, fine, coarse_end[:, depth:-depth], field, links_of(wide_coupling, depth))
        return inward_order(jnp.transpose(end, (1, 0, 2)))[None]

    return shards


def solution(mesh):
    tm, space = mesh.shape["tm"], mesh.shape["space"]
    finer = Mesh(mesh.devices.reshape(tm // 2, 2, 2, space // 2), EVERY)
    rows = ("zh", "rest")
    return jax.shard_map(
        make_shards(tm, space),
        mesh=finer,
        in_specs=(P(rows, None, None), P(rows, None, None), P(rows, None)),
        out_specs=P(("x", "core"), rows, None, None),
        check_vma=False,
    )
```

time: 176 us -> 146 us (0.83)
  Pallas kernels: 137 us -> 123 us
  starting transfers between devices: 17.5 us -> 5.1 us
  waiting for transfers between devices: 6.33 us -> 2.53 us
  other arithmetic: 10.6 us -> 7.79 us
  local copies, waits for them, and re-layouts: 3.52 us -> 5.99 us
    pallas_call x2, Pallas kernels: 137 us -> 123 us  [the longest x1 94.8 us: fine_states(): pl.pallas_call(functools.partial(fine_kernel, space), out_shape=jax.Shape...]
    ppermute x5 -> x3, starting transfers between devices: 17.5 us -> 5.1 us  [shift(): return lax.ppermute(block, ('zh', 'rest'), pairs)]
    ppermute x5 -> x3, waiting for transfers between devices: 6.33 us -> 2.53 us  [shift(): return lax.ppermute(block, ('zh', 'rest'), pairs)]
    rev x0 -> x5, local copies, waits for them, and re-layouts: none -> 2.53 us  [the longest x4 2.34 us: inward_order(): return jnp.where(zh == 1, block[::-1], block)]
  transfers between devices with their start and end apart: 5 -> 3, of which waited for: 2 -> 1; matrix products, arithmetic and copies ran while one was open for 2% -> 1% of each run, Pallas kernels for 0% -> 0%
where the time goes in v1:
time: 146 us; the launch traced here: 145 us
  Pallas kernels  123 us (84%)
  other arithmetic  7.79 us (5%)
  local copies, waits for them, and re-layouts  5.99 us (4%)
  starting transfers between devices  5.1 us (3%)
  waiting for transfers between devices  2.53 us (2%)
    pallas_call x1, Pallas kernels, fine_states(): pl.pallas_call(functools.partial(fine_kernel, space), out_shape=jax.Shape...  94.8 us
    pallas_call x1, Pallas kernels, sweep(): pl.pallas_call(kernel, out_shape=jax.ShapeDtypeStruct(coarse_end.shape, f...  28.5 us
    ppermute x3, starting transfers between devices, shift(): return lax.ppermute(block, ('zh', 'rest'), pairs)  5.1 us
  transfers between devices with their start and end apart: 3, of which 1 were waited for; matrix products, arithmetic and copies ran while one was open for 1% of the time, Pallas kernels for 0%

profile of v1, /device:TPU:3, one launch (start us, length us, event | category | flops | bytes accessed | tf_op | source)
XLA Modules:
  0.0 145.0 jit_solution(6228799083934412391)
XLA Ops:
  0.0 1.9 %rev.15 = f32[64,3,512]{2,0,1:T(8,128)S(1)} reverse(f32[64,3,512]{2,0,1:T(8,128)} %param.9), dimensions={0} | reverse | bytes 786432 | tf_op jit(solution)/shard_map/rev | solution.py:721
  2.1 0.7 copy-done.3
  3.0 0.9 copy-done.2
  4.0 0.7 collective-permute-start.1
  4.7 3.1 %collective-permute-start = (f32[7,4,512]{2,1,0:T(4,128)S(1)}, f32[7,4,512]{2,1,0:T(4,128)S(1)}, u32[]{:S(2)}, u32[]{:S(2)}) collective-permute-start(f32[7,4,512]{2,1,0:T(4,128)S(1)} %get-tuple-element.35), channel_id=1, source_target_pairs={{0,1},{1,2},{2,3},{7,6},{6,5},{5,4},{8,9},{9,10},{10,11},{15,14},{... | collective-permute-start | bytes 172040 | tf_op jit(solution)/shard_map/ppermute | solution.py:728
  7.8 1.3 collective-permute-start.2
  9.1 0.7 slice_select_fusion.1.field
  10.2 2.5 %collective-permute-done.2 = f32[7,4,512]{2,1,0:T(4,128)S(1)} collective-permute-done((f32[7,4,512]{2,1,0:T(4,128)S(1)}, f32[7,4,512]{2,1,0:T(4,128)S(1)}, u32[]{:S(2)}, u32[]{:S(2)}) %collective-permute-start.2) | collective-permute-done | bytes 57376 | tf_op jit(solution)/shard_map/ppermute | solution.py:728
  13.2 0.4 fusion.10
  14.0 0.4 fusion.18
  14.7 0.3 fusion.45
  14.9 0.4 fusion.26
  15.6 0.4 fusion.48
  16.0 0.4 fusion.34
  16.5 0.2 pad_select_fusion
  16.8 0.7 slice_select_fusion.2.theirs
  17.5 0.7 slice_select_fusion.3.mine
  18.3 0.6 pad.48.coupling
  19.0 0.5 fusion.51
  19.5 0.3 pad_select_fusion.2.refs_1_
  19.8 94.8 %shard_map.91.refs_0_ = f32[2,3,32,512]{3,2,1,0:T(8,128)} custom-call(f32[3,32,512]{2,1,0:T(8,128)} %slice_select_fusion.3.mine, f32[3,32,512]{2,1,0:T(8,128)} %slice_select_fusion.2.theirs, f32[3,32,512]{2,1,0:T(8,128)} %slice_select_fusion.1.field, f32[48,512]{1,0:T(8,128)} %pad.48.coupling, bf16[2,256,512]{2,1,0:T(8,128)(2,1)} %constant.52.clone.table_high, ...), custom_call_target="tpu_custom_call" | custom-call | tf_op jit(solution)/shard_map/pallas_call | solution.py:469
  114.6 0.9 copy-done
  115.5 28.5 %shard_map.92 = f32[3,64,512]{2,1,0:T(8,128)S(1)} custom-call(f32[2,3,32,512]{3,2,1,0:T(8,128)S(1)} %copy-done, f32[3,64,512]{2,1,0:T(8,128)S(1)} %pad_select_fusion.2.refs_1_, f32[3,64,512]{2,1,0:T(8,128)S(1)} %get-tuple-element.40.refs_2_, f32[4,64,512]{2,1,0:T(8,128)S(1)} %fusion.3.refs_3_), custom_call_target="tpu_custom_call" | custom-call | tf_op jit(solution)/shard_map/pallas_call | solution.py:676
  144.2 0.8 select_bitcast_fusion
  (35 shorter events, 2.5 us)
Async XLA Ops:
  0.0 1.9 %copy-start.1 = (f32[64,3,512]{2,0,1:T(8,128)S(1)}, f32[64,3,512]{2,0,1:T(8,128)}, u32[]{:S(2)}) copy-start(f32[64,3,512]{2,0,1:T(8,128)} %param.10) | copy-start | bytes 1179652
  1.9 0.9 copy-start.3
  2.8 1.0 copy-start.2
  4.0 6.0 %collective-permute-start.1 = (f32[7,4,512]{2,1,0:T(4,128)S(1)}, f32[7,4,512]{2,1,0:T(4,128)S(1)}, u32[]{:S(2)}, u32[]{:S(2)}) collective-permute-start(f32[7,4,512]{2,1,0:T(4,128)S(1)} %get-tuple-element.35), channel_id=1, source_target_pairs={{3,4},{4,3},{11,12},{12,11},{19,20},{20,19},{27,28},{28,27}} | collective-permute-start | bytes 172040 | tf_op jit(solution)/shard_map/ppermute | solution.py:728
  4.7 8.1 %collective-permute-start = (f32[7,4,512]{2,1,0:T(4,128)S(1)}, f32[7,4,512]{2,1,0:T(4,128)S(1)}, u32[]{:S(2)}, u32[]{:S(2)}) collective-permute-start(f32[7,4,512]{2,1,0:T(4,128)S(1)} %get-tuple-element.35), channel_id=1, source_target_pairs={{0,1},{1,2},{2,3},{7,6},{6,5},{5,4},{8,9},{9,10},{10,11},{15,14},{... | collective-permute-start | bytes 172040 | tf_op jit(solution)/shard_map/ppermute | solution.py:728
  7.8 4.9 %collective-permute-start.2 = (f32[7,4,512]{2,1,0:T(4,128)S(1)}, f32[7,4,512]{2,1,0:T(4,128)S(1)}, u32[]{:S(2)}, u32[]{:S(2)}) collective-permute-start(f32[7,4,512]{2,1,0:T(4,128)S(1)} %get-tuple-element.34), channel_id=1, source_target_pairs={{1,0},{2,1},{3,2},{6,7},{5,6},{4,5},{9,8},{10,9},{11,10},{14,15},{... | collective-permute-start | bytes 172040 | tf_op jit(solution)/shard_map/ppermute | solution.py:728
  114.5 1.0 copy-start

commit v2 on v1

v2 whole, which is shorter than its diff:
```python
import functools
import math

import jax
import jax.numpy as jnp
import numpy as np
from jax import lax
from jax.experimental import pallas as pl
from jax.experimental.pallas import tpu as pltpu
from jax.sharding import Mesh, PartitionSpec as P

FINE = 2
step_time = 0.06
damping = 0.02
stiffness = 0.25
thickness = 8.0
PASSES = 1

EVERY = ("x", "core", "zh", "rest")


def sector_tables(grid):
    half = grid // 2
    place = 2 * np.arange(half) - (grid - 1)
    wave = np.arange(grid)
    odd_wave = np.where(wave == 0, grid, wave)
    turn = 4 * grid

    def angle(k):
        return 2.0 * np.pi / turn * ((place[:, None] * k[None, :]) % turn)

    table = np.stack([np.cos(angle(wave)), np.sin(angle(odd_wave))]).astype(np.float32)
    fold = np.zeros((grid, grid), np.float32)
    for i in range(half):
        fold[i, i] = fold[grid - 1 - i, i] = fold[i, half + i] = 1.0
        fold[grid - 1 - i, half + i] = -1.0
    return table, fold


def halves(table):
    high = table.astype(jnp.bfloat16)
    return [high, (table - high.astype(np.float32)).astype(jnp.bfloat16)]


def split(value):
    high = value.astype(jnp.bfloat16)
    return high, (value - high.astype(jnp.float32)).astype(jnp.bfloat16)


def cross_of(a, b):
    return [a[1] * b[2] - a[2] * b[1], a[2] * b[0] - a[0] * b[2], a[0] * b[1] - a[1] * b[0]]


def product(passes, left, right):
    def one(a, b):
        return jnp.dot(a, b, preferred_element_type=jnp.float32)

    value = one(left[0], right[0])
    if passes > 1:
        value = value + one(left[1], right[0])
    if passes > 2:
        value = value + one(left[0], right[1])
    return value


def put(passes, pair, where, value):
    high, low = split(value)
    pair[0][where] = high
    if passes > 1:
        pair[1][where] = low


HALO = 8


def parareal_kernel(
    space, tm,
    pack, table_high, table_low, turned_high, turned_low, fold, unfold,
    out,
    state, wide_field, wide_coupling, wide_links, halo_in, theirs, coarse_end,
    current, rate, base, probe, demag, far_start, far_field, far_coupling, links, far_links, tensors,
    edge_out, edge_in, wide_high, wide_low, send_xy, send_z, land, back, got_xy, got_z,
    plane_high, plane_low, mixed_high, mixed_low,
    jumps_in, arrived, last_out, last_in,
    halo_sems, swap_sems, edge_sems, send_sems, land_sems, back_sems, got_sems,
    jump_sends, jump_recvs, chain_sends, chain_recvs,
):
    _, rows, grid = pack.shape
    strip = rows // 2
    rest_count = space // 2
    half = grid // 2
    multi = rest_count // 4
    width = grid // multi
    core, zh, rest = lax.axis_index("core"), lax.axis_index("zh"), lax.axis_index("rest")
    axis_x = lax.axis_index("x")
    slice_number = axis_x * 2 + core
    place = zh * rest_count + rest
    order = jnp.where(zh == 0, rest, rest_count - 1 - rest)
    number = 2 * order + core
    unit = rest // multi
    share = rest % multi
    row_odd, column_odd = unit // 2, unit % 2
    outward_place = jnp.where(zh == 0, place + space - 1, place + 1) % space
    inward_place = jnp.where(zh == 0, place + 1, place + space - 1) % space
    first_block, last_block = order == 0, order == rest_count - 1
    mirror = rest_count - 1 - rest

    def at_place(core_index, rest_index):
        return {"core": core_index, "rest": rest_index}

    def owner(index):
        spot = index // 2
        return at_place(index % 2, jnp.where(zh == 0, spot, rest_count - 1 - spot))

    def block_at(where):
        return {"zh": where // rest_count, "rest": where % rest_count}

    def in_slice(which, where):
        return {
            "x": which // 2, "core": which % 2, "zh": where // rest_count, "rest": where % rest_count,
        }

    def remote(source, target, send_sem, recv_sem, where):
        return pltpu.make_async_remote_copy(
            src_ref=source, dst_ref=target, send_sem=send_sem, recv_sem=recv_sem,
            device_id=where, device_id_type=pl.DeviceIdType.MESH,
        )

    barrier = pltpu.get_barrier_semaphore()
    later, earlier = slice_number < tm - 1, slice_number > 0

    def greet(where):
        pl.semaphore_signal(barrier, inc=1, device_id=where, device_id_type=pl.DeviceIdType.MESH)

    def greet_group(k, carry):
        greet(owner((number + k) % space))
        return carry

    lax.fori_loop(1, space, greet_group, 0)
    for k in range(2):
        greet({"core": k, "zh": 1 - zh, "rest": mirror})

    @pl.when(later)
    def _():
        for where in (outward_place, place, inward_place):
            greet(in_slice(slice_number + 1, where))

    @pl.when(earlier)
    def _():
        for where in (outward_place, place, inward_place):
            greet(in_slice(slice_number - 1, where))

    pl.semaphore_wait(barrier, space + 1 + jnp.where(later, 3, 0) + jnp.where(earlier, 3, 0))

    to_outward = remote(
        pack.at[:, pl.ds(0, HALO), :], halo_in.at[1], halo_sems.at[0, 0], halo_sems.at[1, 1], block_at(outward_place)
    )
    inner_slot = jnp.where(last_block, 1, 0)
    to_inward = remote(
        pack.at[:, pl.ds(rows - HALO, HALO), :], halo_in.at[inner_slot],
        halo_sems.at[0, 1], halo_sems.at[1, inner_slot], block_at(inward_place),
    )

    def halo_arrival(slot):
        return remote(
            pack.at[:, pl.ds(0, HALO), :], halo_in.at[slot], halo_sems.at[0, 0], halo_sems.at[1, slot],
            block_at(inward_place),
        )

    @pl.when(jnp.logical_not(first_block))
    def _():
        to_outward.start()

    to_inward.start()

    partner = {"zh": 1 - zh, "rest": mirror}
    core_rows = pl.ds(pl.multiple_of(core * strip, strip), strip)
    top = 2 * HALO

    state[0, :, top : top + rows, :] = pack[0:3]
    wide_field[:, top : top + rows, :] = pack[3:6]
    wide_coupling[top : top + rows, :] = pack[6]

    def fill(i, carry):
        at = pl.multiple_of(i * 64, 64)
        slot_rows = at + lax.broadcasted_iota(jnp.int32, (64, width), 0)
        slot_columns = share * width + lax.broadcasted_iota(jnp.int32, (64, width), 1)
        unit_length = 2.0 * math.pi / (2 * grid)

        def parts(odd_rows, odd_columns):
            rows = jnp.where((slot_rows == 0) & (odd_rows == 1), grid, slot_rows)
            columns = jnp.where((slot_columns == 0) & (odd_columns == 1), grid, slot_columns)
            wave_rows = unit_length * rows.astype(jnp.float32)
            wave_columns = unit_length * columns.astype(jnp.float32)
            squared = wave_rows * wave_rows + wave_columns * wave_columns
            nonzero = squared > 0.0
            safe = jnp.where(nonzero, squared, 1.0)
            scaled = jnp.sqrt(safe) * thickness
            film = jnp.where(nonzero, (1.0 - jnp.exp(-scaled)) / scaled, 1.0)
            weight = jnp.where(slot_rows == 0, 1.0, 2.0) * jnp.where(slot_columns == 0, 1.0, 2.0)
            weight = weight * (-1.0 / (4 * grid * grid))
            return wave_rows, wave_columns, film, (1.0 - film) / safe, weight

        @pl.when(core == 1)
        def _():
            wave_rows, wave_columns, _, in_plane, weight = parts(row_odd, column_odd)
            tensors[0, pl.ds(at, 64), :] = in_plane * wave_columns * wave_columns * weight
            mixed = in_plane * wave_columns * wave_rows * weight
            sign = jnp.where((row_odd == column_odd) == (zh == 0), -1.0, 1.0)
            tensors[2, pl.ds(at, 64), :] = jnp.where((slot_rows == 0) | (slot_columns == 0), 0.0, mixed * sign)
            wave_rows, wave_columns, _, in_plane, weight = parts(1 - row_odd, 1 - column_odd)
            tensors[1, pl.ds(at, 64), :] = in_plane * wave_rows * wave_rows * weight

        @pl.when(core == 0)
        def _():
            _, _, film, _, weight = parts(row_odd, column_odd)
            tensors[0, pl.ds(at, 64), :] = film * weight

        return carry

    lax.fori_loop(0, grid // 64, fill, 0)


    def set_halo(at, slot, lines):
        for r, line in enumerate(lines):
            state[0, :, at + r : at + r + 1, :] = halo_in[slot, 0:3, line : line + 1, :]
            wide_field[:, at + r : at + r + 1, :] = halo_in[slot, 3:6, line : line + 1, :]
            wide_coupling[at + r : at + r + 1, :] = halo_in[slot, 6, line : line + 1, :]

    def set_block(at, slot):
        state[0, :, at : at + HALO, :] = halo_in[slot, 0:3]
        wide_field[:, at : at + HALO, :] = halo_in[slot, 3:6]
        wide_coupling[at : at + HALO, :] = halo_in[slot, 6]

    @pl.when(first_block)
    def _():
        state[0, :, HALO : top, :] = jnp.zeros((3, HALO, grid), jnp.float32)
        wide_field[:, HALO : top, :] = jnp.zeros((3, HALO, grid), jnp.float32)
        wide_coupling[HALO : top, :] = jnp.zeros((HALO, grid), jnp.float32)

    @pl.when(jnp.logical_not(first_block))
    def _():
        halo_arrival(0).wait_recv()
        set_block(HALO, 0)

    halo_arrival(1).wait_recv()

    @pl.when(last_block)
    def _():
        set_halo(top + rows, 1, list(range(HALO))[::-1])

    @pl.when(jnp.logical_not(last_block))
    def _():
        set_block(top + rows, 1)

    for at in (HALO - 1, top + rows + HALO):
        edge = jnp.zeros((1, grid), jnp.float32)
        wide_coupling[at : at + 1, :] = edge
        for n in range(2):
            for c in range(3):
                state[n, c, at : at + 1, :] = edge

    def make_links(target, first, last, source):
        lane = lax.broadcasted_iota(jnp.int32, (8, grid), 1)
        for at in range(first, last, 8):
            centre = source[at : at + 8, :]
            own = stiffness * centre
            target[0, at : at + 8, :] = own * source[at - 1 : at + 7, :]
            target[1, at : at + 8, :] = own * source[at + 1 : at + 9, :]
            target[2, at : at + 8, :] = jnp.where(lane == 0, 0.0, own * pltpu.roll(centre, 1, 1))
            target[3, at : at + 8, :] = jnp.where(lane == grid - 1, 0.0, own * pltpu.roll(centre, grid - 1, 1))

    make_links(wide_links, HALO, top + rows + HALO, wide_coupling)

    def exchange(read, weights, at):
        total = []
        inside = []
        for c in range(3):
            m = read(c, at)
            value = weights[0] * (read(c, at - 1) - m)
            value = value + weights[1] * (read(c, at + 1) - m)
            value = value + weights[2] * (pltpu.roll(m, 1, 1) - m)
            total.append(value + weights[3] * (pltpu.roll(m, grid - 1, 1) - m))
            inside.append(m)
        return inside, total

    def torque_of(inside, effective):
        turned = cross_of(inside, effective)
        again = cross_of(inside, turned)
        return [-(turned[c] + damping * again[c]) * (1.0 / (1.0 + damping * damping)) for c in range(3)]

    def coarse_step(n):
        before, after = n % 2, (n + 1) % 2

        for at in range(HALO, top + rows + HALO, 8):
            weights = [wide_links[k, at : at + 8, :] for k in range(4)]
            inside, total = exchange(lambda c, where: state[before, c, where : where + 8, :], weights, at)
            effective = [total[c] + wide_field[c, at : at + 8, :] for c in range(3)]
            effective[2] = effective[2] - inside[2]
            moved = torque_of(inside, effective)
            for c in range(3):
                state[after, c, at : at + 8, :] = inside[c] + FINE * step_time * moved[c]

    def native(n):
        return state[n % 2, :, pl.ds(pl.multiple_of(top + core * strip, 8), strip), :]

    def step_body(n, carry):
        coarse_step(n)
        return carry

    lax.fori_loop(0, 2 * axis_x, step_body, 0)
    field_source = pack.at[3:6, core_rows, :]
    coupling_source = wide_coupling.at[pl.ds(pl.multiple_of(HALO + core * strip, 8), strip + 2 * HALO), :]
    swaps = [
        remote(source, target, swap_sems.at[0, n], swap_sems.at[1, n], partner)
        for n, (source, target) in enumerate(
            ((theirs, far_start), (field_source, far_field), (coupling_source, far_coupling))
        )
    ]

    @pl.when(zh == 1)
    def _():
        theirs[...] = native(0)
        swaps[0].start()

    @pl.when(zh == 0)
    def _():
        base[0] = native(0)

    coarse_step(0)

    @pl.when(zh == 0)
    def _():
        theirs[...] = native(1)
        swaps[0].start()

    @pl.when(zh == 1)
    def _():
        base[0] = native(1)

    swaps[1].start()
    swaps[2].start()

    @pl.when(core == 0)
    def _():
        coarse_end[...] = state[1, :, top : top + rows, :]

    @pl.when(core == 1)
    def _():
        coarse_step(1)
        coarse_end[...] = state[0, :, top : top + rows, :]


    for k in range(4):
        links[0, k] = wide_links[k, pl.ds(pl.multiple_of(top + core * strip, 8), strip), :]
    swaps[0].wait()
    base[1] = far_start[...]
    current[:, :, 8 : 8 + strip, :] = base[...]
    probe[...] = base[...]

    def to_unit(kind, r):
        target = (rest + r) % rest_count
        if kind == 1:
            source, landing = send_xy.at[target // multi], land.at[:, pl.ds(number * strip, strip), :]
        else:
            source, landing = send_z.at[target // multi], land.at[0, pl.ds(number * strip, strip), :]
        return remote(source, landing, send_sems.at[kind, r], land_sems.at[number], at_place(kind, target))

    def landed(kind, index):
        if kind == 1:
            source, landing = send_xy.at[0], land.at[:, pl.ds(index * strip, strip), :]
        else:
            source, landing = send_z.at[0], land.at[0, pl.ds(index * strip, strip), :]
        return remote(source, landing, send_sems.at[kind, 0], land_sems.at[index], owner(index))

    def to_owner(kind, k):
        index = (number + k) % space
        if kind == 1:
            source, landing = back.at[:, pl.ds(index * strip, strip), :], got_xy.at[rest]
        else:
            source, landing = back.at[0, pl.ds(index * strip, strip), :], got_z.at[rest]
        return remote(source, landing, back_sems.at[k], got_sems.at[kind, rest], owner(index))

    def gotten(kind, r):
        if kind == 1:
            source, landing = back.at[:, pl.ds(0, strip), :], got_xy.at[r]
        else:
            source, landing = back.at[0, pl.ds(0, strip), :], got_z.at[r]
        return remote(source, landing, back_sems.at[0], got_sems.at[kind, r], at_place(kind, r))

    def transform(kind, passes):
        planes = [(row_odd, column_odd), (1 - row_odd, 1 - column_odd)] if kind == 1 else [(row_odd, column_odd)]
        columns = pl.ds(pl.multiple_of(share * width, width), width)
        for n, (_, odd) in enumerate(planes):
            spectrum = product(
                passes, split(land[n]), (table_high[odd, :, columns], table_low[odd, :, columns])
            )
            put(passes, (plane_high, plane_low), n, spectrum)
        step = half

        def mix(i, carry):
            at = pl.multiple_of(i * step, step)
            lines = pl.ds(at, step)
            both = [
                product(
                    passes, (turned_high[odd, lines, :], turned_low[odd, lines, :]), (plane_high[n], plane_low[n])
                )
                for n, (odd, _) in enumerate(planes)
            ]
            if kind == 1:
                cross_term = tensors[2, lines, :]
                values = [
                    tensors[0, lines, :] * both[0] + cross_term * both[1],
                    cross_term * both[0] + tensors[1, lines, :] * both[1],
                ]
            else:
                values = [tensors[0, lines, :] * both[0]]
            for n, value in enumerate(values):
                put(passes, (mixed_high, mixed_low), (n, lines), value)
            return carry

        lax.fori_loop(0, grid // step, mix, 0)
        for n, (odd_rows, odd_columns) in enumerate(planes):
            film = product(
                passes, (table_high[odd_rows], table_low[odd_rows]), (mixed_high[n], mixed_low[n])
            )
            back[n] = product(
                passes, split(film), (turned_high[odd_columns, columns, :], turned_low[odd_columns, columns, :])
            )

    def unit_work(kind, passes):
        @pl.when(core == kind)
        def _():
            def take(k, carry):
                landed(kind, (number + k) % space).wait_recv()
                return carry

            lax.fori_loop(1, space, take, 0)
            transform(kind, passes)

            def push(k, carry):
                to_owner(kind, k).start()
                return carry

            lax.fori_loop(1, space, push, 0)
            own = pl.ds(pl.multiple_of(number * strip, strip), strip)
            if kind == 1:
                got_xy[rest] = back[:, own, :]
            else:
                got_z[rest] = back[0, own, :]

    def unit_end(kind):
        @pl.when(core == kind)
        def _():
            def drain(k, carry):
                to_owner(kind, k).wait_send()
                return carry

            lax.fori_loop(1, space, drain, 0)

    def evaluate(parity, passes, first):
        for t in range(2):
            for c in range(3):
                edge_out[0, 3 * t + c : 3 * t + c + 1, :] = current[t, c, 8:9, :]
                edge_out[1, 3 * t + c : 3 * t + c + 1, :] = current[t, c, 7 + strip : 8 + strip, :]
        outward = remote(
            edge_out.at[0], edge_in.at[parity, 1], edge_sems.at[parity, 0], edge_sems.at[parity, 1], owner((number + space - 1) % space)
        )
        inward = remote(
            edge_out.at[1], edge_in.at[parity, 0], edge_sems.at[parity, 2], edge_sems.at[parity, 3], owner((number + 1) % space)
        )
        fold_passes = min(passes, 2)
        for c in range(3):
            near, far = probe[0, c], probe[1, c]
            for p, value in enumerate((near + far, near - far)):
                put(fold_passes, (wide_high, wide_low), pl.ds((3 * p + c) * strip, strip), value)
        folded = product(fold_passes, (wide_high[...], wide_low[...]), (fold[...],))
        for p in range(2):
            for q in range(2):
                for c in range(3):
                    piece = folded[(3 * p + c) * strip : (3 * p + c + 1) * strip, q * half : (q + 1) * half]
                    if c == 0:
                        send_xy[2 * p + q, 0] = piece
                    elif c == 1:
                        send_xy[2 * (1 - p) + 1 - q, 1] = piece
                    else:
                        send_z[2 * p + q] = piece

        def launch(r, carry):
            for kind in range(2):
                @pl.when((core != kind) | (r != 0))
                def _(kind=kind):
                    to_unit(kind, r).start()

            return carry

        lax.fori_loop(0, rest_count, launch, 0)
        outward.start()
        inward.start()
        own = pl.ds(pl.multiple_of(number * strip, strip), strip)

        @pl.when(core == 1)
        def _():
            land[:, own, :] = send_xy[unit]

        @pl.when(core == 0)
        def _():
            land[0, own, :] = send_z[unit]

        unit_work(1, passes)
        unit_work(0, passes)

        def settle(r, carry):
            for kind in range(2):
                @pl.when((core != kind) | (r != 0))
                def _(kind=kind):
                    to_unit(kind, r).wait_send()
                    gotten(kind, (rest + r) % rest_count).wait_recv()

            return carry

        lax.fori_loop(0, rest_count, settle, 0)
        outward.wait()
        inward.wait()
        for p in range(2):
            for q in range(2):
                for c in range(3):
                    source = 2 * (1 - p) + 1 - q if c == 1 else 2 * p + q
                    value = None
                    for k in range(multi):
                        piece = got_z[source * multi + k] if c == 2 else got_xy[source * multi + k, c]
                        value = piece if value is None else value + piece
                    where = (pl.ds((3 * p + c) * strip, strip), pl.ds(q * half, half))
                    put(fold_passes, (wide_high, wide_low), where, value)
        unfolded = product(fold_passes, (wide_high[...], wide_low[...]), (unfold[...],))
        for c in range(3):
            even = unfolded[c * strip : (c + 1) * strip]
            odd = unfolded[(3 + c) * strip : (4 + c) * strip]
            for t, value in enumerate((even + odd, even - odd)):
                if first:
                    demag[0, t, c] = value
                    demag[1, t, c] = value
                elif parity == 0:
                    moved = demag[0, t, c] + value
                    demag[0, t, c] = moved
                    demag[1, t, c] = moved
                else:
                    demag[1, t, c] = demag[0, t, c] + value
        if first:
            for swap in swaps[1:]:
                swap.wait()
            make_links(far_links, HALO, HALO + strip, far_coupling)
            links[1] = far_links[:, HALO : HALO + strip, :]
        unit_end(1)
        unit_end(0)
        last = number == space - 1
        for t in range(2):
            for c in range(3):
                current[t, c, 7:8, :] = edge_in[parity, 0, 3 * t + c : 3 * t + c + 1, :]
                facing = current[1 - t, c, 7 + strip : 8 + strip, :]
                arrived = edge_in[parity, 1, 3 * t + c : 3 * t + c + 1, :]
                current[t, c, 8 + strip : 9 + strip, :] = jnp.where(last, facing, arrived)
        for t in range(2):
            applied = (wide_field.at[:, pl.ds(pl.multiple_of(top + core * strip, 8), strip), :], far_field)[t]
            for at in range(0, strip, 8):
                rows_here = slice(at, at + 8)
                weights = [links[t, n, rows_here, :] for n in range(4)]
                inside, total = exchange(lambda c, where: current[t, c, where : where + 8, :], weights, 8 + at)
                effective = [total[c] + demag[1, t, c, rows_here, :] + applied[c, rows_here, :] for c in range(3)]
                moved = torque_of(inside, effective)
                for c in range(3):
                    if parity == 0:
                        rate[t, c, rows_here, :] = moved[c]
                        probe[t, c, rows_here, :] = step_time * moved[c]
                    else:
                        change = 0.5 * step_time * (rate[t, c, rows_here, :] + moved[c])
                        probe[t, c, rows_here, :] = change
                        base[t, c, rows_here, :] = base[t, c, rows_here, :] + change
        if parity == 0:
            current[:, :, 8 : 8 + strip, :] = base[...] + probe[...]
        else:
            current[:, :, 8 : 8 + strip, :] = base[...]

    evaluate(0, 3, True)

    def fine_step(i, carry):
        evaluate(1, PASSES, False)
        evaluate(0, PASSES, False)
        return carry

    lax.fori_loop(1, FINE, fine_step, 0)
    evaluate(1, PASSES, False)

    direct = core == zh
    away = {"core": zh, "zh": 1 - zh, "rest": mirror}
    beside = {"core": 1 - core}

    def carry_jump(t, where):
        return remote(base.at[t], jumps_in.at[core], jump_sends.at[t], jump_recvs.at[core], where)

    def await_jump(part):
        remote(base.at[0], jumps_in.at[part], jump_sends.at[0], jump_recvs.at[part], away).wait_recv()

    far, near = carry_jump(1, away), carry_jump(0, beside)
    far.start()

    @pl.when(jnp.logical_not(direct))
    def _():
        near.start()
        await_jump(0)
        await_jump(1)

    @pl.when(direct)
    def _():
        jumps_in[core] = base[0]
        await_jump(1 - core)

    outer = jnp.where(first_block, 0, 1)
    inner = jnp.where(last_block, 1, 0)
    outgoing = [
        remote(source, target, chain_sends.at[n], chain_recvs.at[sem], in_slice(slice_number + 1, where))
        for n, (source, target, sem, where) in enumerate((
            (out, arrived.at[:, pl.ds(8, rows), :], 2, place),
            (last_out.at[0], last_in.at[outer], outer, outward_place),
            (last_out.at[1], last_in.at[inner], inner, inward_place),
        ))
    ]
    arrivals = [
        remote(source, target, chain_sends.at[0], chain_recvs.at[sem], in_slice(slice_number - 1, place))
        for source, target, sem in (
            (out, arrived.at[:, pl.ds(8, rows), :], 2),
            (last_out.at[0], last_in.at[0], 0),
            (last_out.at[1], last_in.at[1], 1),
        )
    ]

    @pl.when(slice_number == 0)
    def _():
        for c in range(3):
            for k in range(2):
                out[c, k * strip : (k + 1) * strip, :] = jumps_in[k, c]

    @pl.when(earlier)
    def _():
        for copy in arrivals:
            copy.wait_recv()
        for c in range(3):
            arrived[c, 7:8, :] = last_in[0, c : c + 1, :]
            arrived[c, 8 + rows : 9 + rows, :] = last_in[1, c : c + 1, :]
        for at in range(0, rows, 8):
            weights = [wide_links[n, top + at : top + at + 8, :] for n in range(4)]
            inside, total = exchange(lambda c, where: arrived[c, where : where + 8, :], weights, 8 + at)
            effective = [total[c] + wide_field[c, top + at : top + at + 8, :] for c in range(3)]
            effective[2] = effective[2] - inside[2]
            moved = torque_of(inside, effective)
            k, within = at // strip, at % strip
            for c in range(3):
                jump = jumps_in[k, c, within : within + 8, :] - coarse_end[c, at : at + 8, :]
                out[c, at : at + 8, :] = inside[c] + FINE * step_time * moved[c] + jump

    @pl.when(later)
    def _():
        for c in range(3):
            last_out[0, c : c + 1, :] = out[c, 0:1, :]
            last_out[1, c : c + 1, :] = out[c, rows - 1 : rows, :]
        for copy in outgoing:
            copy.start()
        for copy in outgoing:
            copy.wait_send()

    far.wait_send()

    @pl.when(jnp.logical_not(direct))
    def _():
        near.wait_send()

    @pl.when(jnp.logical_not(first_block))
    def _():
        to_outward.wait_send()

    to_inward.wait_send()


def parareal(space, tm, pack, tables):
    _, rows, grid = pack.shape
    strip = rows // 2
    half = grid // 2
    rest_count = space // 2
    width = grid * 4 // rest_count
    f32, bf16 = jnp.float32, jnp.bfloat16
    operands = [pack, *tables]
    return pl.pallas_call(
        functools.partial(parareal_kernel, space, tm),
        out_shape=jax.ShapeDtypeStruct((3, rows, grid), f32),
        in_specs=[pl.BlockSpec(memory_space=pltpu.VMEM)] * len(operands),
        out_specs=pl.BlockSpec(memory_space=pltpu.VMEM),
        scratch_shapes=[
            pltpu.VMEM((2, 3, rows + 4 * HALO, grid), f32),
            pltpu.VMEM((3, rows + 4 * HALO, grid), f32),
            pltpu.VMEM((rows + 4 * HALO, grid), f32),
            pltpu.VMEM((4, rows + 4 * HALO, grid), f32),
            pltpu.VMEM((2, 7, HALO, grid), f32),
            pltpu.VMEM((3, strip, grid), f32),
            pltpu.VMEM((3, rows, grid), f32),
            pltpu.VMEM((2, 3, strip + 16, grid), f32),
            pltpu.VMEM((2, 3, strip, grid), f32),
            pltpu.VMEM((2, 3, strip, grid), f32),
            pltpu.VMEM((2, 3, strip, grid), f32),
            pltpu.VMEM((2, 2, 3, strip, grid), f32),
            pltpu.VMEM((3, strip, grid), f32),
            pltpu.VMEM((3, strip, grid), f32),
            pltpu.VMEM((strip + 16, grid), f32),
            pltpu.VMEM((2, 4, strip, grid), f32),
            pltpu.VMEM((4, strip + 16, grid), f32),
            pltpu.VMEM((3, grid, width), f32),
            pltpu.VMEM((2, 8, grid), f32),
            pltpu.VMEM((2, 2, 8, grid), f32),
            pltpu.VMEM((6 * strip, grid), bf16),
            pltpu.VMEM((6 * strip, grid), bf16),
            pltpu.VMEM((4, 2, strip, half), f32),
            pltpu.VMEM((4, strip, half), f32),
            pltpu.VMEM((2, half, half), f32),
            pltpu.VMEM((2, half, half), f32),
            pltpu.VMEM((rest_count, 2, strip, half), f32),
            pltpu.VMEM((rest_count, strip, half), f32),
            pltpu.VMEM((2, half, width), bf16),
            pltpu.VMEM((2, half, width), bf16),
            pltpu.VMEM((2, grid, width), bf16),
            pltpu.VMEM((2, grid, width), bf16),
            pltpu.VMEM((2, 3, strip, grid), f32),
            pltpu.VMEM((3, rows + 16, grid), f32),
            pltpu.VMEM((2, 8, grid), f32),
            pltpu.VMEM((2, 8, grid), f32),
            pltpu.SemaphoreType.DMA((2, 2)),
            pltpu.SemaphoreType.DMA((2, 3)),
            pltpu.SemaphoreType.DMA((2, 4)),
            pltpu.SemaphoreType.DMA((2, rest_count)),
            pltpu.SemaphoreType.DMA((space,)),
            pltpu.SemaphoreType.DMA((space,)),
            pltpu.SemaphoreType.DMA((2, rest_count)),
            pltpu.SemaphoreType.DMA((2,)),
            pltpu.SemaphoreType.DMA((2,)),
            pltpu.SemaphoreType.DMA((3,)),
            pltpu.SemaphoreType.DMA((3,)),
        ],
        compiler_params=pltpu.CompilerParams(
            collective_id=0, has_side_effects=True, vmem_limit_bytes=56 * 1024 * 1024
        ),
    )(*operands)


def make_shards(tm, space):
    def shards(initial_state, applied_field, coupling):
        grid = initial_state.shape[2]
        zh = lax.axis_index("zh")
        table, fold = sector_tables(grid)

        def inward_order(block):
            return jnp.where(zh == 1, block[::-1], block)

        start = jnp.transpose(inward_order(initial_state), (1, 0, 2))
        field = jnp.transpose(inward_order(applied_field), (1, 0, 2))
        pack = jnp.concatenate([start, field, inward_order(coupling)[None]], axis=0)
        tables = [*halves(table), *halves(np.ascontiguousarray(np.transpose(table, (0, 2, 1))))]
        tables += [fold.astype(jnp.bfloat16), np.ascontiguousarray(fold.T).astype(jnp.bfloat16)]
        end = parareal(space, tm, pack, tables)
        return inward_order(jnp.transpose(end, (1, 0, 2)))[None]

    return shards


def solution(mesh):
    tm, space = mesh.shape["tm"], mesh.shape["space"]
    finer = Mesh(mesh.devices.reshape(tm // 2, 2, 2, space // 2), EVERY)
    rows = ("zh", "rest")
    return jax.shard_map(
        make_shards(tm, space),
        mesh=finer,
        in_specs=(P(rows, None, None), P(rows, None, None), P(rows, None)),
        out_specs=P(("x", "core"), rows, None, None),
        check_vma=False,
    )
```

time: 146 us -> 126 us (0.86)
  starting transfers between devices: 5.1 us -> 0 us
  Pallas kernels: 123 us -> 118 us
  other arithmetic: 7.79 us -> 2.89 us
  waiting for transfers between devices: 2.53 us -> 0 us
    ppermute x3 -> x0, starting transfers between devices: 5.1 us -> none  [shift(): return lax.ppermute(block, ('zh', 'rest'), pairs)]
    pallas_call x2 -> x1, Pallas kernels: 123 us -> 118 us  [parareal(): pl.pallas_call(functools.partial(parareal_kernel, space, tm), out_shape=j...]
    add x8 -> x0, other arithmetic: 2.92 us -> none  [the longest x4 1.58 us: coarse(): effective = exchange_field(padded, pad_coupling) + field]
    select_n x7 -> x0, other arithmetic: 2.71 us -> none  [the longest x4 2.17 us: half_of(): return jnp.where(core == 0, low, high)]
    ppermute x3 -> x0, waiting for transfers between devices: 2.53 us -> none  [shift(): return lax.ppermute(block, ('zh', 'rest'), pairs)]
    unnamed x8 -> x6, local copies, waits for them, and re-layouts: 2.51 us -> 0.82 us
    rev x4, local copies, waits for them, and re-layouts: 2.34 us -> 3.84 us  [inward_order(): return jnp.where(zh == 1, block[::-1], block)]
  transfers between devices with their start and end apart: 3 -> 0, of which waited for: 1 -> 0; matrix products, arithmetic and copies ran while one was open for 1% -> 0% of each run, Pallas kernels for 0% -> 0%
where the time goes in v2:
time: 126 us
  Pallas kernels  118 us (94%)
  local copies, waits for them, and re-layouts  4.66 us (4%)
  other arithmetic  2.89 us (2%)
    pallas_call x1, Pallas kernels, parareal(): pl.pallas_call(functools.partial(parareal_kernel, space, tm), out_shape=j...  118 us
    rev x4, local copies, waits for them, and re-layouts, inward_order(): return jnp.where(zh == 1, block[::-1], block)  3.84 us

profile of v2, /device:TPU:3, one launch (start us, length us, event | category | flops | bytes accessed | tf_op | source)
XLA Modules:
  0.0 126.0 jit_solution(8675274807390588556)
XLA Ops:
  0.0 0.0 copy-start.2
  0.0 1.6 %rev.14 = f32[64,512]{1,0:T(8,128)S(1)} reverse(f32[64,512]{1,0:T(8,128)} %param.11), dimensions={0} | reverse | bytes 262144 | tf_op jit(solution)/shard_map/rev | solution.py:759
  1.6 0.9 select_bitcast_fusion.3
  2.5 0.0 copy-done.2
  2.5 0.0 copy-start.1
  2.5 0.2 rev.12
  2.7 0.8 copy-done.1
  3.5 0.2 rev.13
  3.7 0.1 select_bitcast_fusion.1
  3.9 1.0 pad_maximum_fusion.pack
  4.9 118.3 %shard_map.91 = f32[3,64,512]{2,1,0:T(8,128)} custom-call(f32[7,64,512]{2,1,0:T(8,128)} %pad_maximum_fusion.pack, bf16[2,256,512]{2,1,0:T(8,128)(2,1)} %constant.20.clone.table_high, bf16[2,256,512]{2,1,0:T(8,128)(2,1)} %constant.21.clone.table_low, bf16[2,512,256]{2,1,0:T(8,128)(2,1)} %constant.22.clone.turned_high, ...), custom_call_target="tpu_custom_call" | custom-call | tf_op jit(solution)/shard_map/pallas_call | solution.py:692
  123.2 0.0 copy-start
  123.2 1.9 %rev.15 = f32[64,3,512]{2,0,1:T(8,128)S(1)} reverse(f32[64,3,512]{2,0,1:T(8,128)} %bitcast.10), dimensions={0} | reverse | bytes 786432 | tf_op jit(solution)/shard_map/rev | solution.py:759
  125.2 0.0 copy-done
  125.2 0.8 select_bitcast_fusion
Async XLA Ops:
  0.0 2.5 %copy-start.2 = (f32[64,3,512]{2,0,1:T(8,128)S(1)}, f32[64,3,512]{2,0,1:T(8,128)}, u32[]{:S(2)}) copy-start(f32[64,3,512]{2,0,1:T(8,128)} %param.9) | copy-start | bytes 1179652
  2.5 1.0 copy-start.1
  123.2 1.9 %copy-start = (f32[3,64,512]{2,1,0:T(8,128)S(1)}, f32[3,64,512]{2,1,0:T(8,128)}, u32[]{:S(2)}) copy-start(f32[3,64,512]{2,1,0:T(8,128)} %shard_map.91) | copy-start | bytes 1179652

commit v3 on v2

--- a/solution.py
+++ b/solution.py
@@ -70,22 +70,37 @@
         pair[1][where] = low
 
 
+VMEM_LIMIT = 66_600_000
 HALO = 8
+EARLY = 2
+TABLES = 9
 
 
 def parareal_kernel(
     space, tm,
-    pack, table_high, table_low, turned_high, turned_low, fold, unfold,
-    out,
-    state, wide_field, wide_coupling, wide_links, halo_in, theirs, coarse_end,
-    current, rate, base, probe, demag, far_start, far_field, far_coupling, links, far_links, tensors,
-    edge_out, edge_in, wide_high, wide_low, send_xy, send_z, land, back, got_xy, got_z,
-    plane_high, plane_low, mixed_high, mixed_low,
-    jumps_in, arrived, last_out, last_in,
-    halo_sems, swap_sems, edge_sems, send_sems, land_sems, back_sems, got_sems,
-    jump_sends, jump_recvs, chain_sends, chain_recvs,
+    *refs,
 ):
-    _, rows, grid = pack.shape
+    sources, out, rest_refs = refs[:TABLES], refs[TABLES], refs[TABLES + 1 :]
+    copies_in, rest_refs = rest_refs[: TABLES + 1], rest_refs[TABLES + 1 :]
+    (
+        start_in, field_in, coupling_in, table_high, table_low, turned_high, turned_low, fold, unfold, table_sems,
+    ) = copies_in
+    (
+        state, wide_field, wide_coupling, wide_links, halo_out, halo_in, theirs, coarse_end,
+        current, rate, base, probe, demag, far_start, far_field, far_coupling, links, far_links, tensors,
+        edge_out, edge_in, wide_high, wide_low, send, land, back, got,
+        plane_high, plane_low, mixed_high, mixed_low,
+        jumps_in, arrived, last_out, last_in,
+        halo_sems, swap_sems, edge_sems, send_sems, land_sems, back_sems, got_sems,
+        jump_sends, jump_recvs, chain_sends, chain_recvs,
+    ) = rest_refs
+    loads = [
+        pltpu.make_async_copy(source, target, table_sems.at[n])
+        for n, (source, target) in enumerate(zip(sources, copies_in[:TABLES]))
+    ]
+    for load in loads:
+        load.start()
+    _, rows, grid = start_in.shape
     strip = rows // 2
     rest_count = space // 2
     half = grid // 2
@@ -150,20 +165,68 @@
         for where in (outward_place, place, inward_place):
             greet(in_slice(slice_number - 1, where))
 
+    core_rows = pl.ds(pl.multiple_of(2 * HALO + core * strip, 8), strip)
+    top = 2 * HALO
+    tiles = rows // 8
+    sublane = lax.broadcasted_iota(jnp.int32, (8, grid), 0)
+
+    def flipped(value):
+        for k in (1, 2, 4):
+            value = jnp.where(
+                sublane // k % 2 == 1, pltpu.roll(value, k, 0), pltpu.roll(value, 8 - k, 0)
+            )
+        return value
+
+    def natural(c, at):
+        if c < 3:
+            return start_in[c, at : at + 8, :]
+        return field_in[c - 3, at : at + 8, :] if c < 6 else coupling_in[at : at + 8, :]
+
+    def keep(c, at, value):
+        lines = slice(top + at, top + at + 8)
+        if c < 3:
+            state[0, c, lines, :] = value
+        elif c < 6:
+            wide_field[c - 3, lines, :] = value
+        else:
+            wide_coupling[lines, :] = value
+
+    for load in loads[:3]:
+        load.wait()
+
+    @pl.when(zh == 0)
+    def _():
+        for c in range(7):
+            for t in range(tiles):
+                keep(c, 8 * t, natural(c, 8 * t))
+            halo_out[0, c] = natural(c, 0)
+            halo_out[1, c] = natural(c, rows - 8)
+
+    @pl.when(zh == 1)
+    def _():
+        for c in range(7):
+            for t in range(tiles):
+                value = flipped(natural(c, rows - 8 - 8 * t))
+                keep(c, 8 * t, value)
+                if t == 0:
+                    halo_out[0, c] = value
+                if t == tiles - 1:
+                    halo_out[1, c] = value
+
     pl.semaphore_wait(barrier, space + 1 + jnp.where(later, 3, 0) + jnp.where(earlier, 3, 0))
 
     to_outward = remote(
-        pack.at[:, pl.ds(0, HALO), :], halo_in.at[1], halo_sems.at[0, 0], halo_sems.at[1, 1], block_at(outward_place)
+        halo_out.at[0], halo_in.at[1], halo_sems.at[0, 0], halo_sems.at[1, 1], block_at(outward_place)
     )
     inner_slot = jnp.where(last_block, 1, 0)
     to_inward = remote(
-        pack.at[:, pl.ds(rows - HALO, HALO), :], halo_in.at[inner_slot],
+        halo_out.at[1], halo_in.at[inner_slot],
         halo_sems.at[0, 1], halo_sems.at[1, inner_slot], block_at(inward_place),
     )
 
     def halo_arrival(slot):
         return remote(
-            pack.at[:, pl.ds(0, HALO), :], halo_in.at[slot], halo_sems.at[0, 0], halo_sems.at[1, slot],
+            halo_out.at[0], halo_in.at[slot], halo_sems.at[0, 0], halo_sems.at[1, slot],
             block_at(inward_place),
         )
 
@@ -174,12 +237,133 @@
     to_inward.start()
 
     partner = {"zh": 1 - zh, "rest": mirror}
-    core_rows = pl.ds(pl.multiple_of(core * strip, strip), strip)
-    top = 2 * HALO
-
-    state[0, :, top : top + rows, :] = pack[0:3]
-    wide_field[:, top : top + rows, :] = pack[3:6]
-    wide_coupling[top : top + rows, :] = pack[6]
+    coupling_source = wide_coupling.at[pl.ds(pl.multiple_of(HALO + core * strip, 8), strip + 2 * HALO), :]
+    start_swaps = [
+        remote(theirs.at[c], far_start.at[c], swap_sems.at[0, c], swap_sems.at[1, c], partner) for c in range(3)
+    ]
+    field_swaps = [
+        remote(
+            wide_field.at[c, core_rows, :], far_field.at[c], swap_sems.at[0, 3 + c], swap_sems.at[1, 3 + c], partner
+        )
+        for c in range(3)
+    ]
+    coupling_swap = remote(coupling_source, far_coupling, swap_sems.at[0, 6], swap_sems.at[1, 6], partner)
+    for copy in field_swaps[:EARLY]:
+        copy.start()
+
+
+    def set_halo(at, slot, lines):
+        for r, line in enumerate(lines):
+            state[0, :, at + r : at + r + 1, :] = halo_in[slot, 0:3, line : line + 1, :]
+            wide_field[:, at + r : at + r + 1, :] = halo_in[slot, 3:6, line : line + 1, :]
+            wide_coupling[at + r : at + r + 1, :] = halo_in[slot, 6, line : line + 1, :]
+
+    def set_block(at, slot):
+        state[0, :, at : at + HALO, :] = halo_in[slot, 0:3]
+        wide_field[:, at : at + HALO, :] = halo_in[slot, 3:6]
+        wide_coupling[at : at + HALO, :] = halo_in[slot, 6]
+
+    @pl.when(first_block)
+    def _():
+        state[0, :, HALO : top, :] = jnp.zeros((3, HALO, grid), jnp.float32)
+        wide_field[:, HALO : top, :] = jnp.zeros((3, HALO, grid), jnp.float32)
+        wide_coupling[HALO : top, :] = jnp.zeros((HALO, grid), jnp.float32)
+
+    @pl.when(jnp.logical_not(first_block))
+    def _():
+        halo_arrival(0).wait_recv()
+        set_block(HALO, 0)
+
+    halo_arrival(1).wait_recv()
+
+    @pl.when(last_block)
+    def _():
+        set_halo(top + rows, 1, list(range(HALO))[::-1])
+
+    @pl.when(jnp.logical_not(last_block))
+    def _():
+        set_block(top + rows, 1)
+
+    for at in (HALO - 1, top + rows + HALO):
+        edge = jnp.zeros((1, grid), jnp.float32)
+        wide_coupling[at : at + 1, :] = edge
+        for n in range(2):
+            for c in range(3):
+                state[n, c, at : at + 1, :] = edge
+
+    def make_links(target, first, last, source):
+        lane = lax.broadcasted_iota(jnp.int32, (8, grid), 1)
+        for at in range(first, last, 8):
+            centre = source[at : at + 8, :]
+            own = stiffness * centre
+            target[0, at : at + 8, :] = own * source[at - 1 : at + 7, :]
+            target[1, at : at + 8, :] = own * source[at + 1 : at + 9, :]
+            target[2, at : at + 8, :] = jnp.where(lane == 0, 0.0, own * pltpu.roll(centre, 1, 1))
+            target[3, at : at + 8, :] = jnp.where(lane == grid - 1, 0.0, own * pltpu.roll(centre, grid - 1, 1))
+
+    make_links(wide_links, HALO, top + rows + HALO, wide_coupling)
+
+    def exchange(read, weights, at):
+        total = []
+        inside = []
+        for c in range(3):
+            m = read(c, at)
+            value = weights[0] * (read(c, at - 1) - m)
+            value = value + weights[1] * (read(c, at + 1) - m)
+            value = value + weights[2] * (pltpu.roll(m, 1, 1) - m)
+            total.append(value + weights[3] * (pltpu.roll(m, grid - 1, 1) - m))
+            inside.append(m)
+        return inside, total
+
+    def torque_of(inside, effective):
+        turned = cross_of(inside, effective)
+        again = cross_of(inside, turned)
+        return [-(turned[c] + damping * again[c]) * (1.0 / (1.0 + damping * damping)) for c in range(3)]
+
+    def coarse_step(n):
+        before, after = n % 2, (n + 1) % 2
+
+        for at in range(HALO, top + rows + HALO, 8):
+            weights = [wide_links[k, at : at + 8, :] for k in range(4)]
+            inside, total = exchange(lambda c, where: state[before, c, where : where + 8, :], weights, at)
+            effective = [total[c] + wide_field[c, at : at + 8, :] for c in range(3)]
+            effective[2] = effective[2] - inside[2]
+            moved = torque_of(inside, effective)
+            for c in range(3):
+                state[after, c, at : at + 8, :] = inside[c] + FINE * step_time * moved[c]
+
+    def native(n):
+        return state[n % 2, :, pl.ds(pl.multiple_of(top + core * strip, 8), strip), :]
+
+    def step_pair(n, carry):
+        coarse_step(0)
+        coarse_step(1)
+        return carry
+
+    lax.fori_loop(0, axis_x, step_pair, 0)
+    def send_start():
+        for copy in start_swaps:
+            copy.start()
+
+    @pl.when(zh == 1)
+    def _():
+        theirs[...] = native(0)
+        send_start()
+
+    @pl.when(zh == 0)
+    def _():
+        base[0] = native(0)
+
+    coarse_step(0)
+
+    @pl.when(zh == 0)
+    def _():
+        theirs[...] = native(1)
+        send_start()
+
+    @pl.when(zh == 1)
+    def _():
+        base[0] = native(1)
 
     def fill(i, carry):
         at = pl.multiple_of(i * 64, 64)
@@ -220,178 +404,60 @@
 
     lax.fori_loop(0, grid // 64, fill, 0)
 
-
-    def set_halo(at, slot, lines):
-        for r, line in enumerate(lines):
-            state[0, :, at + r : at + r + 1, :] = halo_in[slot, 0:3, line : line + 1, :]
-            wide_field[:, at + r : at + r + 1, :] = halo_in[slot, 3:6, line : line + 1, :]
-            wide_coupling[at + r : at + r + 1, :] = halo_in[slot, 6, line : line + 1, :]
-
-    def set_block(at, slot):
-        state[0, :, at : at + HALO, :] = halo_in[slot, 0:3]
-        wide_field[:, at : at + HALO, :] = halo_in[slot, 3:6]
-        wide_coupling[at : at + HALO, :] = halo_in[slot, 6]
-
-    @pl.when(first_block)
-    def _():
-        state[0, :, HALO : top, :] = jnp.zeros((3, HALO, grid), jnp.float32)
-        wide_field[:, HALO : top, :] = jnp.zeros((3, HALO, grid), jnp.float32)
-        wide_coupling[HALO : top, :] = jnp.zeros((HALO, grid), jnp.float32)
-
-    @pl.when(jnp.logical_not(first_block))
-    def _():
-        halo_arrival(0).wait_recv()
-        set_block(HALO, 0)
-
-    halo_arrival(1).wait_recv()
-
-    @pl.when(last_block)
-    def _():
-        set_halo(top + rows, 1, list(range(HALO))[::-1])
-
-    @pl.when(jnp.logical_not(last_block))
-    def _():
-        set_block(top + rows, 1)
-
-    for at in (HALO - 1, top + rows + HALO):
-        edge = jnp.zeros((1, grid), jnp.float32)
-        wide_coupling[at : at + 1, :] = edge
-        for n in range(2):
-            for c in range(3):
-                state[n, c, at : at + 1, :] = edge
-
-    def make_links(target, first, last, source):
-        lane = lax.broadcasted_iota(jnp.int32, (8, grid), 1)
-        for at in range(first, last, 8):
-            centre = source[at : at + 8, :]
-            own = stiffness * centre
-            target[0, at : at + 8, :] = own * source[at - 1 : at + 7, :]
-            target[1, at : at + 8, :] = own * source[at + 1 : at + 9, :]
-            target[2, at : at + 8, :] = jnp.where(lane == 0, 0.0, own * pltpu.roll(centre, 1, 1))
-            target[3, at : at + 8, :] = jnp.where(lane == grid - 1, 0.0, own * pltpu.roll(centre, grid - 1, 1))
-
-    make_links(wide_links, HALO, top + rows + HALO, wide_coupling)
-
-    def exchange(read, weights, at):
-        total = []
-        inside = []
-        for c in range(3):
-            m = read(c, at)
-            value = weights[0] * (read(c, at - 1) - m)
-            value = value + weights[1] * (read(c, at + 1) - m)
-            value = value + weights[2] * (pltpu.roll(m, 1, 1) - m)
-            total.append(value + weights[3] * (pltpu.roll(m, grid - 1, 1) - m))
-            inside.append(m)
-        return inside, total
-
-    def torque_of(inside, effective):
-        turned = cross_of(inside, effective)
-        again = cross_of(inside, turned)
-        return [-(turned[c] + damping * again[c]) * (1.0 / (1.0 + damping * damping)) for c in range(3)]
-
-    def coarse_step(n):
-        before, after = n % 2, (n + 1) % 2
-
-        for at in range(HALO, top + rows + HALO, 8):
-            weights = [wide_links[k, at : at + 8, :] for k in range(4)]
-            inside, total = exchange(lambda c, where: state[before, c, where : where + 8, :], weights, at)
-            effective = [total[c] + wide_field[c, at : at + 8, :] for c in range(3)]
-            effective[2] = effective[2] - inside[2]
-            moved = torque_of(inside, effective)
-            for c in range(3):
-                state[after, c, at : at + 8, :] = inside[c] + FINE * step_time * moved[c]
-
-    def native(n):
-        return state[n % 2, :, pl.ds(pl.multiple_of(top + core * strip, 8), strip), :]
-
-    def step_body(n, carry):
-        coarse_step(n)
-        return carry
-
-    lax.fori_loop(0, 2 * axis_x, step_body, 0)
-    field_source = pack.at[3:6, core_rows, :]
-    coupling_source = wide_coupling.at[pl.ds(pl.multiple_of(HALO + core * strip, 8), strip + 2 * HALO), :]
-    swaps = [
-        remote(source, target, swap_sems.at[0, n], swap_sems.at[1, n], partner)
-        for n, (source, target) in enumerate(
-            ((theirs, far_start), (field_source, far_field), (coupling_source, far_coupling))
-        )
-    ]
-
-    @pl.when(zh == 1)
-    def _():
-        theirs[...] = native(0)
-        swaps[0].start()
-
-    @pl.when(zh == 0)
-    def _():
-        base[0] = native(0)
-
-    coarse_step(0)
-
-    @pl.when(zh == 0)
-    def _():
-        theirs[...] = native(1)
-        swaps[0].start()
-
-    @pl.when(zh == 1)
-    def _():
-        base[0] = native(1)
-
-    swaps[1].start()
-    swaps[2].start()
-
-    @pl.when(core == 0)
-    def _():
-        coarse_end[...] = state[1, :, top : top + rows, :]
-
-    @pl.when(core == 1)
-    def _():
-        coarse_step(1)
-        coarse_end[...] = state[0, :, top : top + rows, :]
-
-
+    for load in loads[3:]:
+        load.wait()
     for k in range(4):
         links[0, k] = wide_links[k, pl.ds(pl.multiple_of(top + core * strip, 8), strip), :]
-    swaps[0].wait()
-    base[1] = far_start[...]
-    current[:, :, 8 : 8 + strip, :] = base[...]
-    probe[...] = base[...]
-
-    def to_unit(kind, r):
+    current[0, :, 8 : 8 + strip, :] = base[0]
+    probe[0] = base[0]
+
+    own_lines = pl.ds(pl.multiple_of(number * strip, strip), strip)
+
+    def to_unit(plane, r):
+        kind, slot = (1, plane) if plane < 2 else (0, 0)
         target = (rest + r) % rest_count
-        if kind == 1:
-            source, landing = send_xy.at[target // multi], land.at[:, pl.ds(number * strip, strip), :]
-        else:
-            source, landing = send_z.at[target // multi], land.at[0, pl.ds(number * strip, strip), :]
-        return remote(source, landing, send_sems.at[kind, r], land_sems.at[number], at_place(kind, target))
-
-    def landed(kind, index):
-        if kind == 1:
-            source, landing = send_xy.at[0], land.at[:, pl.ds(index * strip, strip), :]
-        else:
-            source, landing = send_z.at[0], land.at[0, pl.ds(index * strip, strip), :]
-        return remote(source, landing, send_sems.at[kind, 0], land_sems.at[index], owner(index))
-
-    def to_owner(kind, k):
+        return remote(
+            send.at[plane, target // multi], land.at[slot, own_lines, :],
+            send_sems.at[plane, r], land_sems.at[slot, number], at_place(kind, target),
+        )
+
+    def landed(slot, index):
+        return remote(
+            send.at[slot, 0], land.at[slot, pl.ds(index * strip, strip), :],
+            send_sems.at[slot, 0], land_sems.at[slot, index], owner(index),
+        )
+
+    def to_owner(plane, k):
+        slot = plane if plane < 2 else 0
         index = (number + k) % space
-        if kind == 1:
-            source, landing = back.at[:, pl.ds(index * strip, strip), :], got_xy.at[rest]
-        else:
-            source, landing = back.at[0, pl.ds(index * strip, strip), :], got_z.at[rest]
-        return remote(source, landing, back_sems.at[k], got_sems.at[kind, rest], owner(index))
-
-    def gotten(kind, r):
-        if kind == 1:
-            source, landing = back.at[:, pl.ds(0, strip), :], got_xy.at[r]
-        else:
-            source, landing = back.at[0, pl.ds(0, strip), :], got_z.at[r]
-        return remote(source, landing, back_sems.at[0], got_sems.at[kind, r], at_place(kind, r))
+        return remote(
+            back.at[slot, pl.ds(index * strip, strip), :], got.at[plane, rest],
+            back_sems.at[slot, k], got_sems.at[plane, rest], owner(index),
+        )
+
+    def gotten(plane, r):
+        kind, slot = (1, plane) if plane < 2 else (0, 0)
+        return remote(
+            back.at[slot, pl.ds(0, strip), :], got.at[plane, r],
+            back_sems.at[slot, 0], got_sems.at[plane, r], at_place(kind, r),
+        )
+
+    def each(first, last, action):
+        def one(k, carry):
+            action(k)
+            return carry
+
+        lax.fori_loop(first, last, one, 0)
+
+    def push(plane):
+        each(1, space, lambda k: to_owner(plane, k).start())
+        got[plane, rest] = back[plane if plane < 2 else 0, own_lines, :]
 
     def transform(kind, passes):
         planes = [(row_odd, column_odd), (1 - row_odd, 1 - column_odd)] if kind == 1 else [(row_odd, column_odd)]
         columns = pl.ds(pl.multiple_of(share * width, width), width)
         for n, (_, odd) in enumerate(planes):
+            each(1, space, lambda k: landed(n, (number + k) % space).wait_recv())
             spectrum = product(
                 passes, split(land[n]), (table_high[odd, :, columns], table_low[odd, :, columns])
             )
@@ -427,115 +493,79 @@
             back[n] = product(
                 passes, split(film), (turned_high[odd_columns, columns, :], turned_low[odd_columns, columns, :])
             )
+            push(n if kind == 1 else 2)
 
     def unit_work(kind, passes):
         @pl.when(core == kind)
         def _():
-            def take(k, carry):
-                landed(kind, (number + k) % space).wait_recv()
-                return carry
-
-            lax.fori_loop(1, space, take, 0)
             transform(kind, passes)
-
-            def push(k, carry):
-                to_owner(kind, k).start()
-                return carry
-
-            lax.fori_loop(1, space, push, 0)
-            own = pl.ds(pl.multiple_of(number * strip, strip), strip)
-            if kind == 1:
-                got_xy[rest] = back[:, own, :]
-            else:
-                got_z[rest] = back[0, own, :]
 
     def unit_end(kind):
         @pl.when(core == kind)
         def _():
-            def drain(k, carry):
-                to_owner(kind, k).wait_send()
-                return carry
-
-            lax.fori_loop(1, space, drain, 0)
+            for plane in (0, 1) if kind == 1 else (2,):
+                each(1, space, lambda k: to_owner(plane, k).wait_send())
+
+    def elsewhere(plane, r, action):
+        pl.when((core != (1 if plane < 2 else 0)) | (r != 0))(action)
 
     def evaluate(parity, passes, first):
+        outward = remote(
+            edge_out.at[0], edge_in.at[parity, 1], edge_sems.at[parity, 0], edge_sems.at[parity, 1],
+            owner((number + space - 1) % space),
+        )
+        inward = remote(
+            edge_out.at[1], edge_in.at[parity, 0], edge_sems.at[parity, 2], edge_sems.at[parity, 3],
+            owner((number + 1) % space),
+        )
+        fold_passes = min(passes, 2)
+        for c in range(3):
+            if first:
+                start_swaps[c].wait()
+                base[1, c] = far_start[c]
+                probe[1, c] = far_start[c]
+                current[1, c, 8 : 8 + strip, :] = far_start[c]
+            near, far = probe[0, c], probe[1, c]
+            lines = pl.ds(2 * c * strip, 2 * strip)
+            for p, value in enumerate((near + far, near - far)):
+                put(fold_passes, (wide_high, wide_low), pl.ds((2 * c + p) * strip, strip), value)
+            folded = product(fold_passes, (wide_high[lines, :], wide_low[lines, :]), (fold[...],))
+            for p in range(2):
+                for q in range(2):
+                    which = 2 * (1 - p) + 1 - q if c == 1 else 2 * p + q
+                    send[c, which] = folded[p * strip : (p + 1) * strip, q * half : (q + 1) * half]
+            each(0, rest_count, lambda r: elsewhere(c, r, lambda: to_unit(c, r).start()))
+
+            @pl.when(core == (1 if c < 2 else 0))
+            def _():
+                land[c if c < 2 else 0, own_lines, :] = send[c, unit]
+
         for t in range(2):
             for c in range(3):
                 edge_out[0, 3 * t + c : 3 * t + c + 1, :] = current[t, c, 8:9, :]
                 edge_out[1, 3 * t + c : 3 * t + c + 1, :] = current[t, c, 7 + strip : 8 + strip, :]
-        outward = remote(
-            edge_out.at[0], edge_in.at[parity, 1], edge_sems.at[parity, 0], edge_sems.at[parity, 1], owner((number + space - 1) % space)
-        )
-        inward = remote(
-            edge_out.at[1], edge_in.at[parity, 0], edge_sems.at[parity, 2], edge_sems.at[parity, 3], owner((number + 1) % space)
-        )
-        fold_passes = min(passes, 2)
-        for c in range(3):
-            near, far = probe[0, c], probe[1, c]
-            for p, value in enumerate((near + far, near - far)):
-                put(fold_passes, (wide_high, wide_low), pl.ds((3 * p + c) * strip, strip), value)
-        folded = product(fold_passes, (wide_high[...], wide_low[...]), (fold[...],))
-        for p in range(2):
-            for q in range(2):
-                for c in range(3):
-                    piece = folded[(3 * p + c) * strip : (3 * p + c + 1) * strip, q * half : (q + 1) * half]
-                    if c == 0:
-                        send_xy[2 * p + q, 0] = piece
-                    elif c == 1:
-                        send_xy[2 * (1 - p) + 1 - q, 1] = piece
-                    else:
-                        send_z[2 * p + q] = piece
-
-        def launch(r, carry):
-            for kind in range(2):
-                @pl.when((core != kind) | (r != 0))
-                def _(kind=kind):
-                    to_unit(kind, r).start()
-
-            return carry
-
-        lax.fori_loop(0, rest_count, launch, 0)
         outward.start()
         inward.start()
-        own = pl.ds(pl.multiple_of(number * strip, strip), strip)
-
-        @pl.when(core == 1)
-        def _():
-            land[:, own, :] = send_xy[unit]
-
-        @pl.when(core == 0)
-        def _():
-            land[0, own, :] = send_z[unit]
-
+        if first:
+            for copy in field_swaps[EARLY:]:
+                copy.start()
+            coupling_swap.start()
         unit_work(1, passes)
         unit_work(0, passes)
-
-        def settle(r, carry):
-            for kind in range(2):
-                @pl.when((core != kind) | (r != 0))
-                def _(kind=kind):
-                    to_unit(kind, r).wait_send()
-                    gotten(kind, (rest + r) % rest_count).wait_recv()
-
-            return carry
-
-        lax.fori_loop(0, rest_count, settle, 0)
-        outward.wait()
-        inward.wait()
-        for p in range(2):
-            for q in range(2):
-                for c in range(3):
+        for c in (2, 0, 1):
+            each(0, rest_count, lambda r: elsewhere(c, r, lambda: gotten(c, (rest + r) % rest_count).wait_recv()))
+            lines = pl.ds(2 * c * strip, 2 * strip)
+            for p in range(2):
+                for q in range(2):
                     source = 2 * (1 - p) + 1 - q if c == 1 else 2 * p + q
                     value = None
                     for k in range(multi):
-                        piece = got_z[source * multi + k] if c == 2 else got_xy[source * multi + k, c]
+                        piece = got[c, source * multi + k]
                         value = piece if value is None else value + piece
-                    where = (pl.ds((3 * p + c) * strip, strip), pl.ds(q * half, half))
+                    where = (pl.ds((2 * c + p) * strip, strip), pl.ds(q * half, half))
                     put(fold_passes, (wide_high, wide_low), where, value)
-        unfolded = product(fold_passes, (wide_high[...], wide_low[...]), (unfold[...],))
-        for c in range(3):
-            even = unfolded[c * strip : (c + 1) * strip]
-            odd = unfolded[(3 + c) * strip : (4 + c) * strip]
+            unfolded = product(fold_passes, (wide_high[lines, :], wide_low[lines, :]), (unfold[...],))
+            even, odd = unfolded[:strip], unfolded[strip:]
             for t, value in enumerate((even + odd, even - odd)):
                 if first:
                     demag[0, t, c] = value
@@ -546,9 +576,13 @@
                     demag[1, t, c] = moved
                 else:
                     demag[1, t, c] = demag[0, t, c] + value
+        for c in range(3):
+            each(0, rest_count, lambda r: elsewhere(c, r, lambda: to_unit(c, r).wait_send()))
+        outward.wait()
+        inward.wait()
         if first:
-            for swap in swaps[1:]:
-                swap.wait()
+            for copy in [*field_swaps, coupling_swap]:
+                copy.wait()
             make_links(far_links, HALO, HALO + strip, far_coupling)
             links[1] = far_links[:, HALO : HALO + strip, :]
         unit_end(1)
@@ -607,6 +641,18 @@
     @pl.when(jnp.logical_not(direct))
     def _():
         near.start()
+
+    @pl.when(core == 0)
+    def _():
+        coarse_end[...] = state[1, :, top : top + rows, :]
+
+    @pl.when(core == 1)
+    def _():
+        coarse_step(1)
+        coarse_end[...] = state[0, :, top : top + rows, :]
+
+    @pl.when(jnp.logical_not(direct))
+    def _():
         await_jump(0)
         await_jump(1)
 
@@ -680,25 +726,37 @@
 
     to_inward.wait_send()
 
-
-def parareal(space, tm, pack, tables):
-    _, rows, grid = pack.shape
+    @pl.when(zh == 1)
+    def _():
+        for c in range(3):
+            for t in range(tiles // 2):
+                low, high = slice(8 * t, 8 * t + 8), slice(rows - 8 - 8 * t, rows - 8 * t)
+                upper, lower = flipped(out[c, high, :]), flipped(out[c, low, :])
+                out[c, low, :] = upper
+                out[c, high, :] = lower
+
+
+def parareal(space, tm, start, field, coupling, tables):
+    _, rows, grid = start.shape
     strip = rows // 2
     half = grid // 2
     rest_count = space // 2
     width = grid * 4 // rest_count
     f32, bf16 = jnp.float32, jnp.bfloat16
-    operands = [pack, *tables]
+    operands = [start, field, coupling, *tables]
     return pl.pallas_call(
         functools.partial(parareal_kernel, space, tm),
         out_shape=jax.ShapeDtypeStruct((3, rows, grid), f32),
-        in_specs=[pl.BlockSpec(memory_space=pltpu.VMEM)] * len(operands),
+        in_specs=[pl.BlockSpec(memory_space=pl.ANY)] * TABLES,
         out_specs=pl.BlockSpec(memory_space=pltpu.VMEM),
         scratch_shapes=[
+            *(pltpu.VMEM(operand.shape, operand.dtype) for operand in operands),
+            pltpu.SemaphoreType.DMA((TABLES,)),
             pltpu.VMEM((2, 3, rows + 4 * HALO, grid), f32),
             pltpu.VMEM((3, rows + 4 * HALO, grid), f32),
             pltpu.VMEM((rows + 4 * HALO, grid), f32),
             pltpu.VMEM((4, rows + 4 * HALO, grid), f32),
+            pltpu.VMEM((2, 7, HALO, grid), f32),
             pltpu.VMEM((2, 7, HALO, grid), f32),
             pltpu.VMEM((3, strip, grid), f32),
             pltpu.VMEM((3, rows, grid), f32),
@@ -717,12 +775,10 @@
             pltpu.VMEM((2, 2, 8, grid), f32),
             pltpu.VMEM((6 * strip, grid), bf16),
             pltpu.VMEM((6 * strip, grid), bf16),
-            pltpu.VMEM((4, 2, strip, half), f32),
-            pltpu.VMEM((4, strip, half), f32),
+            pltpu.VMEM((3, 4, strip, half), f32),
             pltpu.VMEM((2, half, half), f32),
             pltpu.VMEM((2, half, half), f32),
-            pltpu.VMEM((rest_count, 2, strip, half), f32),
-            pltpu.VMEM((rest_count, strip, half), f32),
+            pltpu.VMEM((3, rest_count, strip, half), f32),
             pltpu.VMEM((2, half, width), bf16),
             pltpu.VMEM((2, half, width), bf16),
             pltpu.VMEM((2, grid, width), bf16),
@@ -732,19 +788,19 @@
             pltpu.VMEM((2, 8, grid), f32),
             pltpu.VMEM((2, 8, grid), f32),
             pltpu.SemaphoreType.DMA((2, 2)),
-            pltpu.SemaphoreType.DMA((2, 3)),
+            pltpu.SemaphoreType.DMA((2, 7)),
             pltpu.SemaphoreType.DMA((2, 4)),
-            pltpu.SemaphoreType.DMA((2, rest_count)),
-            pltpu.SemaphoreType.DMA((space,)),
-            pltpu.SemaphoreType.DMA((space,)),
-            pltpu.SemaphoreType.DMA((2, rest_count)),
+            pltpu.SemaphoreType.DMA((3, rest_count)),
+            pltpu.SemaphoreType.DMA((2, space)),
+            pltpu.SemaphoreType.DMA((2, space)),
+            pltpu.SemaphoreType.DMA((3, rest_count)),
             pltpu.SemaphoreType.DMA((2,)),
             pltpu.SemaphoreType.DMA((2,)),
             pltpu.SemaphoreType.DMA((3,)),
             pltpu.SemaphoreType.DMA((3,)),
         ],
         compiler_params=pltpu.CompilerParams(
-            collective_id=0, has_side_effects=True, vmem_limit_bytes=56 * 1024 * 1024
+            collective_id=0, has_side_effects=True, vmem_limit_bytes=VMEM_LIMIT
         ),
     )(*operands)
 
@@ -752,19 +808,13 @@
 def make_shards(tm, space):
     def shards(initial_state, applied_field, coupling):
         grid = initial_state.shape[2]
-        zh = lax.axis_index("zh")
         table, fold = sector_tables(grid)
-
-        def inward_order(block):
-            return jnp.where(zh == 1, block[::-1], block)
-
-        start = jnp.transpose(inward_order(initial_state), (1, 0, 2))
-        field = jnp.transpose(inward_order(applied_field), (1, 0, 2))
-        pack = jnp.concatenate([start, field, inward_order(coupling)[None]], axis=0)
+        start = jnp.transpose(initial_state, (1, 0, 2))
+        field = jnp.transpose(applied_field, (1, 0, 2))
         tables = [*halves(table), *halves(np.ascontiguousarray(np.transpose(table, (0, 2, 1))))]
         tables += [fold.astype(jnp.bfloat16), np.ascontiguousarray(fold.T).astype(jnp.bfloat16)]
-        end = parareal(space, tm, pack, tables)
-        return inward_order(jnp.transpose(end, (1, 0, 2)))[None]
+        end = parareal(space, tm, start, field, coupling, tables)
+        return jnp.transpose(end, (1, 0, 2))[None]
 
     return shards
 

time: 126 us -> 113 us (0.90)
  Pallas kernels: 118 us -> 111 us
  other arithmetic: 2.89 us -> 0 us
  local copies, waits for them, and re-layouts: 4.66 us -> 1.77 us
    pallas_call x1, Pallas kernels: 118 us -> 111 us  [parareal(): pl.pallas_call(functools.partial(parareal_kernel, space, tm), out_shape=j...]
    rev x4 -> x0, local copies, waits for them, and re-layouts: 3.84 us -> none  [inward_order(): return jnp.where(zh == 1, block[::-1], block)]
    broadcast_in_dim x2 -> x0, other arithmetic: 1.73 us -> none  [the longest x1 0.92 us: shards(): pack = jnp.concatenate([start, field, inward_order(coupling)[None]], axis=0)]
where the time goes in v3:
time: 113 us; the launch traced here: 112 us
  Pallas kernels  111 us (98%)
  local copies, waits for them, and re-layouts  1.77 us (2%)
    pallas_call x1, Pallas kernels, parareal(): pl.pallas_call(functools.partial(parareal_kernel, space, tm), out_shape=j...  111 us

profile of v3, /device:TPU:3, one launch (start us, length us, event | category | flops | bytes accessed | tf_op | source)
XLA Modules:
  0.0 112.5 jit_solution(1593490349571840161)
XLA Ops:
  0.0 110.7 %shard_map.91 = f32[3,64,512]{2,1,0:T(8,128)} custom-call(f32[3,64,512]{2,1,0:T(8,128)} %bitcast.6, f32[3,64,512]{2,1,0:T(8,128)} %bitcast.7, f32[64,512]{1,0:T(8,128)} %refs_2_.1, bf16[2,256,512]{2,1,0:T(8,128)(2,1)} %constant.12.clone.refs_3_, bf16[2,256,512]{2,1,0:T(8,128)(2,1)} %constant.13.clone.refs_4_, bf16[2,512,256]{2,1,0:T(8,128)(2,1)} %constant.14.clone.refs_5_, ...), custom_call_target="tpu_custom_call" | custom-call | tf_op jit(solution)/shard_map/pallas_call | solution.py:747
  110.7 1.8 %copy.11 = f32[1,64,3,512]{3,1,2,0:T(8,128)} copy(f32[1,64,3,512]{3,1,2,0:T(8,128)} %bitcast.5) | data formatting | bytes 786432

commit v4 on v3

--- a/solution.py
+++ b/solution.py
@@ -413,9 +413,12 @@
 
     own_lines = pl.ds(pl.multiple_of(number * strip, strip), strip)
 
+    def across(r):
+        return (rest // 2 + r // 2) % (rest_count // 2) * 2 + (rest + r) % 2
+
     def to_unit(plane, r):
         kind, slot = (1, plane) if plane < 2 else (0, 0)
-        target = (rest + r) % rest_count
+        target = across(r)
         return remote(
             send.at[plane, target // multi], land.at[slot, own_lines, :],
             send_sems.at[plane, r], land_sems.at[slot, number], at_place(kind, target),
@@ -429,7 +432,9 @@
 
     def to_owner(plane, k):
         slot = plane if plane < 2 else 0
-        index = (number + k) % space
+        target = across(k // 2)
+        spot = jnp.where(zh == 0, target, rest_count - 1 - target)
+        index = 2 * spot + (core + k) % 2
         return remote(
             back.at[slot, pl.ds(index * strip, strip), :], got.at[plane, rest],
             back_sems.at[slot, k], got_sems.at[plane, rest], owner(index),
@@ -450,7 +455,7 @@
         lax.fori_loop(first, last, one, 0)
 
     def push(plane):
-        each(1, space, lambda k: to_owner(plane, k).start())
+        each(0, space - 1, lambda k: to_owner(plane, space - 1 - k).start())
         got[plane, rest] = back[plane if plane < 2 else 0, own_lines, :]
 
     def transform(kind, passes):
@@ -509,7 +514,7 @@
     def elsewhere(plane, r, action):
         pl.when((core != (1 if plane < 2 else 0)) | (r != 0))(action)
 
-    def evaluate(parity, passes, first):
+    def evaluate(parity, passes, first, last_one=None):
         outward = remote(
             edge_out.at[0], edge_in.at[parity, 1], edge_sems.at[parity, 0], edge_sems.at[parity, 1],
             owner((number + space - 1) % space),
@@ -534,7 +539,9 @@
                 for q in range(2):
                     which = 2 * (1 - p) + 1 - q if c == 1 else 2 * p + q
                     send[c, which] = folded[p * strip : (p + 1) * strip, q * half : (q + 1) * half]
-            each(0, rest_count, lambda r: elsewhere(c, r, lambda: to_unit(c, r).start()))
+            each(0, rest_count, lambda r: elsewhere(
+                c, rest_count - 1 - r, lambda: to_unit(c, rest_count - 1 - r).start()
+            ))
 
             @pl.when(core == (1 if c < 2 else 0))
             def _():
@@ -594,7 +601,7 @@
                 facing = current[1 - t, c, 7 + strip : 8 + strip, :]
                 arrived = edge_in[parity, 1, 3 * t + c : 3 * t + c + 1, :]
                 current[t, c, 8 + strip : 9 + strip, :] = jnp.where(last, facing, arrived)
-        for t in range(2):
+        for t in (1, 0):
             applied = (wide_field.at[:, pl.ds(pl.multiple_of(top + core * strip, 8), strip), :], far_field)[t]
             for at in range(0, strip, 8):
                 rows_here = slice(at, at + 8)
@@ -610,6 +617,8 @@
                         change = 0.5 * step_time * (rate[t, c, rows_here, :] + moved[c])
                         probe[t, c, rows_here, :] = change
                         base[t, c, rows_here, :] = base[t, c, rows_here, :] + change
+            if t == 1 and last_one is not None:
+                last_one()
         if parity == 0:
             current[:, :, 8 : 8 + strip, :] = base[...] + probe[...]
         else:
@@ -623,8 +632,6 @@
         return carry
 
     lax.fori_loop(1, FINE, fine_step, 0)
-    evaluate(1, PASSES, False)
-
     direct = core == zh
     away = {"core": zh, "zh": 1 - zh, "rest": mirror}
     beside = {"core": 1 - core}
@@ -636,7 +643,7 @@
         remote(base.at[0], jumps_in.at[part], jump_sends.at[0], jump_recvs.at[part], away).wait_recv()
 
     far, near = carry_jump(1, away), carry_jump(0, beside)
-    far.start()
+    evaluate(1, PASSES, False, far.start)
 
     @pl.when(jnp.logical_not(direct))
     def _():
@@ -680,11 +687,21 @@
         )
     ]
 
+    def send_edges():
+        @pl.when(later)
+        def _():
+            for c in range(3):
+                last_out[0, c : c + 1, :] = out[c, 0:1, :]
+                last_out[1, c : c + 1, :] = out[c, rows - 1 : rows, :]
+            outgoing[1].start()
+            outgoing[2].start()
+
     @pl.when(slice_number == 0)
     def _():
         for c in range(3):
             for k in range(2):
                 out[c, k * strip : (k + 1) * strip, :] = jumps_in[k, c]
+        send_edges()
 
     @pl.when(earlier)
     def _():
@@ -693,7 +710,8 @@
         for c in range(3):
             arrived[c, 7:8, :] = last_in[0, c : c + 1, :]
             arrived[c, 8 + rows : 9 + rows, :] = last_in[1, c : c + 1, :]
-        for at in range(0, rows, 8):
+
+        def advance(at):
             weights = [wide_links[n, top + at : top + at + 8, :] for n in range(4)]
             inside, total = exchange(lambda c, where: arrived[c, where : where + 8, :], weights, 8 + at)
             effective = [total[c] + wide_field[c, top + at : top + at + 8, :] for c in range(3)]
@@ -704,13 +722,15 @@
                 jump = jumps_in[k, c, within : within + 8, :] - coarse_end[c, at : at + 8, :]
                 out[c, at : at + 8, :] = inside[c] + FINE * step_time * moved[c] + jump
 
+        advance(0)
+        advance(rows - 8)
+        send_edges()
+        for at in range(8, rows - 8, 8):
+            advance(at)
+
     @pl.when(later)
     def _():
-        for c in range(3):
-            last_out[0, c : c + 1, :] = out[c, 0:1, :]
-            last_out[1, c : c + 1, :] = out[c, rows - 1 : rows, :]
-        for copy in outgoing:
-            copy.start()
+        outgoing[0].start()
         for copy in outgoing:
             copy.wait_send()
 

time: 113 us -> 108 us (0.956)
  Pallas kernels: 111 us -> 105 us
    pallas_call x1, Pallas kernels: 111 us -> 105 us  [parareal(): pl.pallas_call(functools.partial(parareal_kernel, space, tm), out_shape=j...]
where the time goes in v4:
time: 108 us; the launch traced here: 107 us
  Pallas kernels  105 us (97%)
  local copies, waits for them, and re-layouts  1.77 us (2%)
    pallas_call x1, Pallas kernels, parareal(): pl.pallas_call(functools.partial(parareal_kernel, space, tm), out_shape=j...  105 us

profile of v4, /device:TPU:3, one launch (start us, length us, event | category | flops | bytes accessed | tf_op | source)
XLA Modules:
  0.0 106.7 jit_solution(6580910674288073750)
XLA Ops:
  0.0 104.9 %shard_map.91 = f32[3,64,512]{2,1,0:T(8,128)} custom-call(f32[3,64,512]{2,1,0:T(8,128)} %bitcast.6, f32[3,64,512]{2,1,0:T(8,128)} %bitcast.7, f32[64,512]{1,0:T(8,128)} %refs_2_.1, bf16[2,256,512]{2,1,0:T(8,128)(2,1)} %constant.12.clone.refs_3_, bf16[2,256,512]{2,1,0:T(8,128)(2,1)} %constant.13.clone.refs_4_, bf16[2,512,256]{2,1,0:T(8,128)(2,1)} %constant.14.clone.refs_5_, ...), custom_call_target="tpu_custom_call" | custom-call | tf_op jit(solution)/shard_map/pallas_call | solution.py:767
  104.9 1.8 %copy.11 = f32[1,64,3,512]{3,1,2,0:T(8,128)} copy(f32[1,64,3,512]{3,1,2,0:T(8,128)} %bitcast.5) | data formatting | bytes 786432

commit v5 on v4

--- a/solution.py
+++ b/solution.py
@@ -199,8 +199,8 @@
         for c in range(7):
             for t in range(tiles):
                 keep(c, 8 * t, natural(c, 8 * t))
-            halo_out[0, c] = natural(c, 0)
-            halo_out[1, c] = natural(c, rows - 8)
+            halo_out[0, tm * c : tm * c + tm, :] = natural(c, 0)[:tm]
+            halo_out[1, tm * c : tm * c + tm, :] = natural(c, rows - 8)[8 - tm :]
 
     @pl.when(zh == 1)
     def _():
@@ -209,9 +209,9 @@
                 value = flipped(natural(c, rows - 8 - 8 * t))
                 keep(c, 8 * t, value)
                 if t == 0:
-                    halo_out[0, c] = value
+                    halo_out[0, tm * c : tm * c + tm, :] = value[:tm]
                 if t == tiles - 1:
-                    halo_out[1, c] = value
+                    halo_out[1, tm * c : tm * c + tm, :] = value[8 - tm :]
 
     pl.semaphore_wait(barrier, space + 1 + jnp.where(later, 3, 0) + jnp.where(earlier, 3, 0))
 
@@ -252,16 +252,15 @@
         copy.start()
 
 
-    def set_halo(at, slot, lines):
-        for r, line in enumerate(lines):
-            state[0, :, at + r : at + r + 1, :] = halo_in[slot, 0:3, line : line + 1, :]
-            wide_field[:, at + r : at + r + 1, :] = halo_in[slot, 3:6, line : line + 1, :]
-            wide_coupling[at + r : at + r + 1, :] = halo_in[slot, 6, line : line + 1, :]
-
-    def set_block(at, slot):
-        state[0, :, at : at + HALO, :] = halo_in[slot, 0:3]
-        wide_field[:, at : at + HALO, :] = halo_in[slot, 3:6]
-        wide_coupling[at : at + HALO, :] = halo_in[slot, 6]
+    def set_halo(at, slot, backwards):
+        for c in range(7):
+            target = (state.at[0, c] if c < 3 else None, wide_field.at[c - 3] if 3 <= c < 6 else None, wide_coupling)[min(c // 3, 2)]
+            if backwards:
+                for r in range(tm):
+                    line = tm * c + tm - 1 - r
+                    target[at + r : at + r + 1, :] = halo_in[slot, line : line + 1, :]
+            else:
+                target[at : at + tm, :] = halo_in[slot, tm * c : tm * c + tm, :]
 
     @pl.when(first_block)
     def _():
@@ -272,17 +271,17 @@
     @pl.when(jnp.logical_not(first_block))
     def _():
         halo_arrival(0).wait_recv()
-        set_block(HALO, 0)
+        set_halo(top - tm, 0, False)
 
     halo_arrival(1).wait_recv()
 
     @pl.when(last_block)
     def _():
-        set_halo(top + rows, 1, list(range(HALO))[::-1])
+        set_halo(top + rows, 1, True)
 
     @pl.when(jnp.logical_not(last_block))
     def _():
-        set_block(top + rows, 1)
+        set_halo(top + rows, 1, False)
 
     for at in (HALO - 1, top + rows + HALO):
         edge = jnp.zeros((1, grid), jnp.float32)
@@ -583,8 +582,6 @@
                     demag[1, t, c] = moved
                 else:
                     demag[1, t, c] = demag[0, t, c] + value
-        for c in range(3):
-            each(0, rest_count, lambda r: elsewhere(c, r, lambda: to_unit(c, r).wait_send()))
         outward.wait()
         inward.wait()
         if first:
@@ -592,8 +589,6 @@
                 copy.wait()
             make_links(far_links, HALO, HALO + strip, far_coupling)
             links[1] = far_links[:, HALO : HALO + strip, :]
-        unit_end(1)
-        unit_end(0)
         last = number == space - 1
         for t in range(2):
             for c in range(3):
@@ -623,6 +618,10 @@
             current[:, :, 8 : 8 + strip, :] = base[...] + probe[...]
         else:
             current[:, :, 8 : 8 + strip, :] = base[...]
+        for c in range(3):
+            each(0, rest_count, lambda r: elsewhere(c, r, lambda: to_unit(c, r).wait_send()))
+        unit_end(1)
+        unit_end(0)
 
     evaluate(0, 3, True)
 
@@ -776,8 +775,8 @@
             pltpu.VMEM((3, rows + 4 * HALO, grid), f32),
             pltpu.VMEM((rows + 4 * HALO, grid), f32),
             pltpu.VMEM((4, rows + 4 * HALO, grid), f32),
-            pltpu.VMEM((2, 7, HALO, grid), f32),
-            pltpu.VMEM((2, 7, HALO, grid), f32),
+            pltpu.VMEM((2, -(-7 * tm // 8) * 8, grid), f32),
+            pltpu.VMEM((2, -(-7 * tm // 8) * 8, grid), f32),
             pltpu.VMEM((3, strip, grid), f32),
             pltpu.VMEM((3, rows, grid), f32),
             pltpu.VMEM((2, 3, strip + 16, grid), f32),

time: 108 us -> 107 us (level)
    pallas_call x1, Pallas kernels: 105 us -> 104 us  [parareal(): pl.pallas_call(functools.partial(parareal_kernel, space, tm), out_shape=j...]
where the time goes in v5:
time: 107 us; the launch traced here: 106 us
  Pallas kernels  104 us (97%)
  local copies, waits for them, and re-layouts  1.77 us (2%)
    pallas_call x1, Pallas kernels, parareal(): pl.pallas_call(functools.partial(parareal_kernel, space, tm), out_shape=j...  104 us

profile of v5, /device:TPU:3, one launch (start us, length us, event | category | flops | bytes accessed | tf_op | source)
XLA Modules:
  0.0 105.5 jit_solution(5444782260570892133)
XLA Ops:
  0.0 103.7 %shard_map.91 = f32[3,64,512]{2,1,0:T(8,128)} custom-call(f32[3,64,512]{2,1,0:T(8,128)} %bitcast.6, f32[3,64,512]{2,1,0:T(8,128)} %bitcast.7, f32[64,512]{1,0:T(8,128)} %refs_2_.1, bf16[2,256,512]{2,1,0:T(8,128)(2,1)} %constant.12.clone.refs_3_, bf16[2,256,512]{2,1,0:T(8,128)(2,1)} %constant.13.clone.refs_4_, bf16[2,512,256]{2,1,0:T(8,128)(2,1)} %constant.14.clone.refs_5_, ...), custom_call_target="tpu_custom_call" | custom-call | tf_op jit(solution)/shard_map/pallas_call | solution.py:766
  103.8 1.8 %copy.11 = f32[1,64,3,512]{3,1,2,0:T(8,128)} copy(f32[1,64,3,512]{3,1,2,0:T(8,128)} %bitcast.5) | data formatting | bytes 786432
